TPU v7x, 32 devices: a whole 2x2x4 slice. The times are simulated.
32 devices in a mesh: vocab: 8 (over z, y), docs: 4 (over x, core).
Axes of the slice: x: 2, y: 2, z: 4, core: 2. Of those that a mesh axis runs over, the one named last changes fastest.
Arguments:
- images: bfloat16 [32768, 4096], P(('vocab', 'docs')), may hold values from -1000 to 1000
- sketch: bfloat16 [4096, 512], replicated, may hold values from -0.09375 to 0.09375
- tile_vals: bfloat16 [32, 32, 2, 64, 128], P(('vocab', 'docs')), as said below
- tile_rows: int32 [32, 32, 2, 64], P(('vocab', 'docs')), may hold values from 0 to 1023
- tile_count: int32 [32, 32], P(('vocab', 'docs')), may hold values from 1 to 2, as said below
- tile_block: int32 [32, 32, 2], P(('vocab', 'docs')), may hold values from 0 to 15
Outputs:
- basis: float32 [65536, 512], P(('vocab', 'docs'))
- factor: float32 [512, 512], replicated
Inputs may be any that keep to these rules, and one draw needn't show every extreme that they name: Slots at index tile_count or above hold values that belong to no tile. In every draw some owners receive 2 live slots from every device. `tile_vals`: nonnegative term weights.
All inputs are finite; a program needn't handle non-finite values.
Results may differ from a plain program's by a relative error of at most 0.003.
The roundings to bfloat16 on the way count: a program that leaves them out, or rounds other values in their place, can miss the bound.
Values may be sent and summed in bfloat16 or wider, within the bound.
No kernel may reach another device: no remote copies, remote signals or barrier semaphores. Data moves between devices by JAX's collectives and lax.ppermute only.
A program may use at most 192 MiB of HBM per device.

v0:
```python
import math

import jax
import jax.numpy as jnp
from jax import lax
from jax.sharding import PartitionSpec as P

VOCAB_DEV = 2048


def collect(totals, pieces):
    summed, squares = totals
    slot_vals, slot_rows, slot_hot = pieces
    product = jnp.einsum("srk,srj->skj", slot_vals, slot_rows, preferred_element_type=jnp.float32)
    summed = summed + jnp.einsum("sb,skj->bkj", slot_hot, product, precision=lax.Precision.HIGHEST)
    weights = slot_vals.astype(jnp.float32)
    powers = jnp.sum(weights * weights, axis=1)
    squares = squares + jnp.einsum("sb,sk->bk", slot_hot, powers, precision=lax.Precision.HIGHEST)
    return ((summed, squares), None)


def body(images, sketch, tile_vals, tile_rows, tile_count, tile_block):
    along_vocab = lax.axis_size("vocab")
    along_docs = lax.axis_size("docs")
    senders = along_vocab * along_docs
    doc_rows = images.shape[0]
    capacity = tile_vals.shape[2]
    tile_height = tile_vals.shape[3]
    tile_width = tile_vals.shape[4]
    columns = sketch.shape[1]
    slot_index = lax.broadcasted_iota(jnp.int32, (senders, capacity), 1)
    alive_mask = slot_index < tile_count[0][:, None]
    outgoing = jnp.where(alive_mask[:, :, None, None], tile_vals[0], jnp.zeros((), jnp.bfloat16))
    feature_sums = jnp.sum(jnp.square(images.astype(jnp.float32)), axis=0)
    feature_sums = lax.psum(feature_sums, ("vocab", "docs"))
    scales = lax.rsqrt(feature_sums / (doc_rows * senders) + 1e-05)
    sketch_scaled = (sketch.astype(jnp.float32) * scales[:, None]).astype(jnp.bfloat16)
    projected = jnp.dot(images, sketch_scaled, preferred_element_type=jnp.float32).astype(
        jnp.bfloat16
    )
    picked = projected[tile_rows[0]]
    arrived_vals, arrived_rows = (
        lax.all_to_all(outgoing, ("vocab", "docs"), split_axis=0, concat_axis=0, tiled=True),
        lax.all_to_all(picked, ("vocab", "docs"), split_axis=0, concat_axis=0, tiled=True),
    )
    slots = senders * capacity
    block_count = VOCAB_DEV // tile_width
    block_ids = tile_block[0].reshape(slots)
    slot_hot = (
        block_ids[:, None] == lax.broadcasted_iota(jnp.int32, (slots, block_count), 1)
    ).astype(jnp.float32)
    bundle = 32
    turns = slots // bundle
    pieces = (
        arrived_vals.reshape(turns, bundle, tile_height, tile_width),
        arrived_rows.reshape(turns, bundle, tile_height, columns),
        slot_hot.reshape(turns, bundle, block_count),
    )
    initial = (
        jnp.zeros((block_count, tile_width, columns), jnp.float32),
        jnp.zeros((block_count, tile_width), jnp.float32),
    )
    (summed, squares), unused = lax.scan(collect, initial, pieces)
    sketch_rows = (summed * lax.rsqrt(squares + 1.0)[:, :, None]).reshape(
        block_count * tile_width, columns
    )
    gram_first = lax.psum(
        jnp.dot(sketch_rows.T, sketch_rows, precision=lax.Precision.HIGHEST), ("vocab", "docs")
    )
    lower_first = jnp.linalg.cholesky(gram_first)
    basis_first = jax.scipy.linalg.solve_triangular(lower_first, sketch_rows.T, lower=True)
    root = math.sqrt(sketch_rows.shape[0] * senders)
    factor = lower_first.T / root
    return (basis_first.T * root, factor)


def solution(mesh):
    placed = (
        P(("vocab", "docs"), None),
        P(),
        P(("vocab", "docs"), None, None, None, None),
        P(("vocab", "docs"), None, None, None),
        P(("vocab", "docs"), None),
        P(("vocab", "docs"), None, None),
    )
    return jax.shard_map(
        body,
        mesh=mesh,
        in_specs=placed,
        out_specs=(P(("vocab", "docs"), None), P()),
        check_vma=False,
    )
```

profile of v0, /device:TPU:0, one launch (start us, length us, event | category | flops | bytes accessed | tf_op | source)
XLA Modules:
  0.0 545.7 jit_solution(18416616957307186575)
XLA Ops:
  10.2 7.3 %all-to-all-start = ((bf16[32,2,64,128]{3,2,1,0:T(8,128)(2,1)}), bf16[32,2,64,128]{3,2,1,0:T(8,128)(2,1)S(1)}, u32[]{:S(2)}, u32[]{:S(2)}) async-start(bf16[32,2,64,128]{3,2,1,0:T(8,128)(2,1)} %bitcast_select_fusion), calls=%async_computation | async-start | bytes 2097152 | tf_op jit(solution)/shard_map/all_to_all | solution.py:43
  17.6 5.1 multiply_reduce_fusion.1
  22.6 41.3 %psum.14 = f32[4096]{0:T(1024)S(1)} all-reduce(f32[4096]{0:T(1024)S(1)} %multiply_reduce_fusion.1), channel_id=1, replica_groups=mesh['vocab'=8,'docs'=4] {'vocab','docs'}, use_global_device_ids=true, to_apply=%region_1.2 | all-reduce | flops 4096 | bytes 32768 | tf_op jit(solution)/shard_map/psum | solution.py:35
  64.0 10.0 %fusion.32 = bf16[1024,512]{0,1:T(8,128)(2,1)S(1)} fusion(bf16[1024,4096]{1,0:T(8,128)(2,1)} %param.8, bf16[4096,512]{1,0:T(8,128)(2,1)} %param.9, f32[4096]{0:T(1024)S(1)} %add_rsqrt_fusion), kind=kOutput, calls=%fused_computation.40 | convolution fusion | flops 4301783040 | bytes 13647872 | tf_op jit(solution)/shard_map/dot_general | solution.py:38
  74.6 17.3 %gather_fusion = bf16[4096,512]{1,0:T(8,128)(2,1)} fusion(bf16[1024,512]{1,0:T(8,128)(2,1)S(1)} %copy.18, s32[4096]{0:T(1024)S(1)} %broadcast_clamp_fusion), kind=kCustom, calls=%fused_computation | custom fusion | bytes 8404992 | tf_op jit(solution)/shard_map/gather | solution.py:41
  97.0 93.1 %all-to-all-done.1 = bf16[32,2,64,512]{3,2,1,0:T(8,128)(2,1)} async-done(((bf16[32,2,64,512]{3,2,1,0:T(8,128)(2,1)}), bf16[32,2,64,512]{3,2,1,0:T(8,128)(2,1)}, u32[]{:S(2)}, u32[]{:S(2)}) %all-to-all-start.1) | async-done | bytes 4194336 | tf_op jit(solution)/shard_map/all_to_all | solution.py:44
  190.2 41.6 %while.15 = (s32[]{:T(128)}, f32[16,128,512]{2,0,1:T(8,128)}, f32[16,128]{1,0:T(8,128)S(1)}, f32[2,32,16]{1,2,0:T(8,128)S(1)}, bf16[2,32,64,128]{3,2,1,0:T(8,128...) while((s32[]{:T(128)}, f32[16,128,512]{2,0,1:T(8,128)}, ...), condition=%wide.region_4.5_spmd.clone, body=%wide.region_2.4_spmd.clone.sunk | while | flops 674758656 | bytes 28378216 | solution.py:63
  190.2 6.1 %fusion.82 = f32[32,128,512]{2,1,0:T(8,128)} fusion(bf16[2,32,64,512]{3,2,1,0:T(8,128)(2,1)} %get-tuple-element.195, s32[]{:T(128)} %get-tuple-element.182, bf16[2,32,64,128]{3,2,1,0:T(8,128)(2,1)S(1)} %get-tuple-element.194), kind=kOutput, calls=%fused_computation.6.clone.1 | convolution fusion | flops 268435456 | bytes 11011072 | tf_op jit(solution)/shard_map/while/body/eval_jaxpr/srk,srj->skj/dot_general | solution.py:14
  196.3 13.8 %select_add_fusion.2 = f32[16,128,512]{2,0,1:T(8,128)} fusion(f32[16,128,512]{2,0,1:T(8,128)} %get-tuple-element.183, f32[32,128,512]{2,1,0:T(8,128)} %fusion.82, pred[]{:T(512)S(6)} %compare.46, f32[2,32,16]{1,2,0:T(8,128)S(1)} %get-tuple-element.193, s32[]{:T(128)} %get-tuple-element.182), kind=kOutput, calls=%fused_computation.5.clone.1 | convolution fusion | flops 404750336 | bytes 16785412 | tf_op jit(solution)/shard_map/while/body/eval_jaxpr/sb,skj->bkj/dot_general | solution.py:15
  210.4 6.1 %fusion.82 = f32[32,128,512]{2,1,0:T(8,128)} fusion(bf16[2,32,64,512]{3,2,1,0:T(8,128)(2,1)} %get-tuple-element.195, s32[]{:T(128)} %get-tuple-element.182, bf16[2,32,64,128]{3,2,1,0:T(8,128)(2,1)S(1)} %get-tuple-element.194), kind=kOutput, calls=%fused_computation.6.clone.1 | convolution fusion | flops 268435456 | bytes 11011072 | tf_op jit(solution)/shard_map/while/body/eval_jaxpr/srk,srj->skj/dot_general | solution.py:14
  216.5 14.5 %select_add_fusion.2 = f32[16,128,512]{2,0,1:T(8,128)} fusion(f32[16,128,512]{2,0,1:T(8,128)} %get-tuple-element.183, f32[32,128,512]{2,1,0:T(8,128)} %fusion.82, pred[]{:T(512)S(6)} %compare.46, f32[2,32,16]{1,2,0:T(8,128)S(1)} %get-tuple-element.193, s32[]{:T(128)} %get-tuple-element.182), kind=kOutput, calls=%fused_computation.5.clone.1 | convolution fusion | flops 404750336 | bytes 16785412 | tf_op jit(solution)/shard_map/while/body/eval_jaxpr/sb,skj->bkj/dot_general | solution.py:15
  238.5 7.8 %convolution_bitcast_fusion = f32[512,512]{0,1:T(8,128)} fusion(f32[16,128,512]{2,1,0:T(8,128)S(1)} %copy_multiply_fusion), kind=kOutput, calls=%fused_computation.41 | convolution fusion | flops 6442450944 | bytes 5242880 | tf_op jit(solution)/shard_map/dot_general | solution.py:68
  246.3 130.4 %all-reduce.3.cloned.1.call-done = f32[512,512]{0,1:T(8,128)} async-done(((f32[512,512]{0,1:T(8,128)}), f32[512,512]{0,1:T(8,128)}) %all-reduce.3.cloned.1.call-update) | async-done | bytes 1048592 | tf_op jit(solution)/shard_map/psum | solution.py:67
  379.8 11.9 %cholesky.104 = f32[128,128]{1,0:T(8,128)S(1)} custom-call(f32[128,128]{1,0:T(8,128)S(1)} %cholesky.266), custom_call_target="Cholesky" | custom-call | tf_op jit(solution)/shard_map/jit(cholesky)/cholesky | solution.py:70
  391.7 9.8 %custom-call.31 = f32[1,128,128]{1,2,0:T(8,128)S(1)} custom-call(f32[1,128,128]{2,1,0:T(8,128)S(1)} %get-tuple-element.103), custom_call_target="InvertDiagBlocksLowerTriangular" | custom-call | tf_op jit(solution)/shard_map/jit(cholesky)/cholesky | solution.py:70
  402.3 11.7 %cholesky.217 = f32[128,128]{1,0:T(8,128)S(1)} custom-call(f32[128,128]{1,0:T(8,128)S(1)} %cholesky.270), custom_call_target="Cholesky" | custom-call | tf_op jit(solution)/shard_map/jit(cholesky)/cholesky | solution.py:70
  414.0 9.8 %custom-call.32 = f32[1,128,128]{1,2,0:T(8,128)S(1)} custom-call(f32[1,128,128]{2,1,0:T(8,128)S(1)} %get-tuple-element.100), custom_call_target="InvertDiagBlocksLowerTriangular" | custom-call | tf_op jit(solution)/shard_map/jit(cholesky)/cholesky | solution.py:70
  424.5 11.9 %cholesky.238 = f32[128,128]{1,0:T(8,128)S(1)} custom-call(f32[128,128]{1,0:T(8,128)S(1)} %cholesky.275), custom_call_target="Cholesky" | custom-call | tf_op jit(solution)/shard_map/jit(cholesky)/cholesky | solution.py:70
  437.2 9.8 %custom-call.33 = f32[1,128,128]{1,2,0:T(8,128)S(1)} custom-call(f32[1,128,128]{2,1,0:T(8,128)S(1)} %get-tuple-element.97), custom_call_target="InvertDiagBlocksLowerTriangular" | custom-call | tf_op jit(solution)/shard_map/jit(cholesky)/cholesky | solution.py:70
  447.6 11.7 %cholesky.255 = f32[128,128]{1,0:T(8,128)S(1)} custom-call(f32[128,128]{1,0:T(8,128)S(1)} %convolution_subtract_fusion.4), custom_call_target="Cholesky" | custom-call | tf_op jit(solution)/shard_map/jit(cholesky)/cholesky | solution.py:70
  463.5 8.5 %while.14 = (s32[]{:T(128)}, f32[512,512]{1,0:T(8,128)S(1)}, s32[4,2]{0,1:T(2,128)S(1)}, f32[4,128,128]{2,1,0:T(8,128)S(1)}, s32[]{:T(128)}) while((s32[]{:T(128)}, f32[512,512]{1,0:T(8,128)S(1)}, s32[4,2]{0,1:T(2,128)S(1)}, f32[4,128,128]{2,1,0:T(8,128)S(1)}, s32[]{:T(128)}) %tuple.54), condition=%wide.while_cond, body=%wide.while_body.sunk | while | flops 2 | bytes 131181 | solution.py:71
  472.0 39.7 %custom-call.34 = f32[4,128,128]{1,2,0:T(8,128)S(1)} custom-call(f32[4,128,128]{2,1,0:T(8,128)S(1)} %get-tuple-element.44), custom_call_target="InvertDiagBlocksLowerTriangular" | custom-call | tf_op jit(solution)/shard_map/jit(_solve_triangular)/triangular_solve | solution.py:71
  522.9 5.5 %fusion.25 = f32[128,2048]{0,1:T(8,128)S(1)} fusion(f32[128,2048]{1,0:T(8,128)S(1)} %fusion.46, f32[128,2048]{1,0:T(8,128)S(1)} %fusion.48, f32[128,2048]{1,0:T(8,128)S(1)} %fusion.33, f32[512,2048]{0,1:T(8,128)S(1)} %bitcast.101, f32[512,512]{1,0:T(8,128)S(1)} %get-tuple-element.220), kind=kOutput, calls=%fused_computation.33 | convolution fusion | flops 1209794560 | bytes 5439488 | tf_op jit(solution)/shard_map/jit(_solve_triangular)/triangular_solve | solution.py:71
  532.0 5.3 copy.23
  (73 shorter events, 48.0 us)
Async XLA Ops:
  10.2 81.7 %all-to-all-start = ((bf16[32,2,64,128]{3,2,1,0:T(8,128)(2,1)}), bf16[32,2,64,128]{3,2,1,0:T(8,128)(2,1)S(1)}, u32[]{:S(2)}, u32[]{:S(2)}) async-start(bf16[32,2,64,128]{3,2,1,0:T(8,128)(2,1)} %bitcast_select_fusion), calls=%async_computation | async-start | bytes 2097152 | tf_op jit(solution)/shard_map/all_to_all | solution.py:43
  64.0 10.5 %copy-start.2 = (s32[1,32,2,64]{3,2,1,0:T(2,128)S(1)}, s32[1,32,2,64]{3,2,1,0:T(2,128)}, u32[]{:S(2)}) copy-start(s32[1,32,2,64]{3,2,1,0:T(2,128)} %param.11) | copy-start | bytes 49156
  91.9 5.0 copy-start.3
  91.9 98.3 %all-to-all-start.1 = ((bf16[32,2,64,512]{3,2,1,0:T(8,128)(2,1)}), bf16[32,2,64,512]{3,2,1,0:T(8,128)(2,1)}, u32[]{:S(2)}, u32[]{:S(2)}) async-start(bf16[32,2,64,512]{3,2,1,0:T(8,128)(2,1)} %bitcast.103), calls=%async_computation.1 | async-start | bytes 8388608 | tf_op jit(solution)/shard_map/all_to_all | solution.py:44
  96.5 280.2 %all-reduce.3.cloned.1.call-start = ((), (), s32[]{:S(2)}) async-start(), calls=%async_computation.2 | async-start | bytes 2097152 | tf_op jit(solution)/shard_map/psum | solution.py:67
  236.4 2.0 copy-start
  511.7 6.6 %copy-start.1 = (f32[16,128,512]{2,1,0:T(8,128)S(1)}, f32[16,128,512]{2,1,0:T(8,128)}, u32[]{:S(2)}) copy-start(f32[16,128,512]{2,1,0:T(8,128)} %copy-done) | copy-start | bytes 12582916
Sparse Core Ops, SparseCore 0:
  246.4 130.2 all-reduce.2
where the time goes:
time: 553 us; the launch traced here: 546 us
  waiting for transfers between devices  224 us (41%)
  other arithmetic  136 us (25%)
  matrix products  78.2 us (14%)
  blocking collectives  41.3 us (7%)
  local copies, waits for them, and re-layouts  36.8 us (7%)
  between operations  17.1 us (3%)
  starting transfers between devices  12.2 us (2%)
    psum x1, waiting for transfers between devices, body(): lax.psum(jnp.dot(sketch_rows.T, sketch_rows, precision=lax.Precision.HIGH...  130 us
    all_to_all x1, waiting for transfers between devices, body(): lax.all_to_all(picked, ('vocab', 'docs'), split_axis=0, concat_axis=0, ti...  93.1 us
    another operation x14, other arithmetic, body(): lower_first = jnp.linalg.cholesky(gram_first)  78.8 us
    psum x1, blocking collectives, body(): feature_sums = lax.psum(feature_sums, ('vocab', 'docs'))  41.3 us
    another operation x2, other arithmetic, body(): jax.scipy.linalg.solve_triangular(lower_first, sketch_rows.T, lower=True)  39.7 us
    dot_general x2, matrix products, collect(): jnp.einsum('sb,skj->bkj', slot_hot, product, precision=lax.Precision.HIGH...  28.3 us
    another operation x7, matrix products, body(): jax.scipy.linalg.solve_triangular(lower_first, sketch_rows.T, lower=True)  17.7 us
    gather x1, local copies, waits for them, and re-layouts, body(): picked = projected[tile_rows[0]]  17.3 us
  transfers between devices with their start and end apart: 3, of which 2 were waited for; matrix products, arithmetic and copies ran while one was open for 6% of the time, Pallas kernels for 0%

commit v1 on v0

v1 whole, which is shorter than its diff:
```python
import math

import jax
import jax.numpy as jnp
from jax import lax
from jax.experimental import pallas as pl
from jax.experimental.pallas import tpu as pltpu
from jax.sharding import PartitionSpec as P


VOCAB_DEV = 2048
LANES = 128
FIRST_PART = 3
BOTH = ("half", "rest", "docs")
SIDE = ("rest", "docs")
F32 = jnp.float32
BF16 = jnp.bfloat16
FULL_VMEM = pl.BlockSpec(memory_space=pltpu.VMEM)
IN_HBM = pl.BlockSpec(memory_space=pltpu.HBM)
IN_SMEM = pl.BlockSpec(memory_space=pltpu.SMEM)


def cost(micros, moved=0):
    return pl.CostEstimate(flops=int(micros * 1e9), bytes_accessed=moved, transcendentals=0)


def params(mebibytes):
    return pltpu.CompilerParams(vmem_limit_bytes=mebibytes * 1024 * 1024)


def split2(x):
    high = x.astype(BF16)
    return high, (x - high.astype(F32)).astype(BF16)


def split3(x):
    high = x.astype(BF16).astype(F32)
    rest = x - high
    middle = rest.astype(BF16).astype(F32)
    return high, middle, rest - middle


def dot(a, b, ca, cb):
    return lax.dot_general(a, b, (((ca,), (cb,)), ((), ())), preferred_element_type=F32)


def exact(a, b, ca, cb):
    return lax.dot_general(
        a, b, (((ca,), (cb,)), ((), ())), preferred_element_type=F32, precision=lax.Precision.HIGHEST
    )


def prepare_kernel(steps, count_ref, images_hbm, vals_hbm, out_ref, power_ref, images_ref, vals_ref, arrivals):
    docs, features = images_ref.shape
    rows = docs // steps
    copies = [pltpu.make_async_copy(vals_hbm.at[0], vals_ref, arrivals.at[steps])]
    for i in range(steps):
        at = pl.ds(i * rows, rows)
        copies.append(pltpu.make_async_copy(images_hbm.at[at], images_ref.at[at], arrivals.at[i]))
    for copy in copies:
        copy.start()
    copies[0].wait()
    senders, capacity = vals_ref.shape[:2]

    def mask(o, carry):
        live = count_ref[0, o]
        for c in range(capacity):
            out_ref[o, c] = vals_ref[o, c] * jnp.where(c < live, 1.0, 0.0).astype(BF16)
        return carry

    lax.fori_loop(0, senders, mask, 0)
    wide = 1024
    totals = [jnp.zeros((8, wide), F32) for _ in range(features // wide)]
    for i in range(steps):
        copies[1 + i].wait()
        for f in range(features // wide):

            def group(r, total):
                at = pl.multiple_of(i * rows + r * 32, 32)
                values = images_ref[pl.ds(at, 32), f * wide : (f + 1) * wide].astype(F32)
                values = values * values
                return total + ((values[:8] + values[8:16]) + (values[16:24] + values[24:]))

            totals[f] = lax.fori_loop(0, rows // 32, group, totals[f])
    for f in range(features // wide):
        power_ref[:, f * wide : (f + 1) * wide] = jnp.sum(totals[f], axis=0, keepdims=True)


def prepare(count, images, vals):
    docs, features = images.shape
    steps = 8
    return pl.pallas_call(
        lambda *refs: prepare_kernel(steps, *refs),
        in_specs=[IN_SMEM, IN_HBM, IN_HBM],
        out_specs=(FULL_VMEM, FULL_VMEM),
        out_shape=(
            jax.ShapeDtypeStruct(vals.shape[1:], BF16),
            jax.ShapeDtypeStruct((1, features), F32),
        ),
        scratch_shapes=[
            pltpu.VMEM((docs, features), BF16),
            pltpu.VMEM(vals.shape[1:], BF16),
            pltpu.SemaphoreType.DMA((steps + 1,)),
        ],
        compiler_params=params(58),
        cost_estimate=cost(4),
        name="prepare",
    )(count, images, vals)


def project_kernel(
    documents, steps, power_ref, images_hbm, sketch_hbm, first_ref, second_ref, images_ref, sketch_ref, scaled_ref, arrivals
):
    features, columns = sketch_ref.shape
    docs = images_ref.shape[0]
    rows = docs // steps
    deep = features // steps
    copies = []
    for i in range(steps):
        at = pl.ds(i * deep, deep)
        copies.append(pltpu.make_async_copy(sketch_hbm.at[at], sketch_ref.at[at], arrivals.at[i]))
    for i in range(steps):
        at = pl.ds(i * rows, rows)
        copies.append(pltpu.make_async_copy(images_hbm.at[at], images_ref.at[at], arrivals.at[steps + i]))
    for copy in copies:
        copy.start()
    for i in range(steps):
        copies[i].wait()
        for k in range(i * deep, (i + 1) * deep, LANES):
            scale = lax.rsqrt(power_ref[:, k : k + LANES] / documents + 1e-05)
            scale = jnp.broadcast_to(scale, (LANES, LANES)).T
            scale = jnp.concatenate([scale] * (columns // LANES), axis=1)
            scaled_ref[k : k + LANES, :] = (sketch_ref[k : k + LANES, :].astype(F32) * scale).astype(BF16)
    cut = first_ref.shape[1]
    for i in range(steps):
        copies[steps + i].wait()
        at = slice(i * rows, (i + 1) * rows)
        found = jnp.dot(images_ref[at, :], scaled_ref[...], preferred_element_type=F32).astype(BF16)
        first_ref[at, :] = found[:, :cut]
        second_ref[at, :] = found[:, cut:]


def project(power, images, sketch, documents, cut):
    docs = images.shape[0]
    _, columns = sketch.shape
    steps = 4
    return pl.pallas_call(
        lambda *refs: project_kernel(documents, steps, *refs),
        in_specs=[FULL_VMEM, IN_HBM, IN_HBM],
        out_specs=(FULL_VMEM, FULL_VMEM),
        out_shape=(
            jax.ShapeDtypeStruct((docs, cut), BF16),
            jax.ShapeDtypeStruct((docs, columns - cut), BF16),
        ),
        scratch_shapes=[
            pltpu.VMEM(images.shape, BF16),
            pltpu.VMEM(sketch.shape, BF16),
            pltpu.VMEM(sketch.shape, BF16),
            pltpu.SemaphoreType.DMA((2 * steps,)),
        ],
        compiler_params=params(58),
        cost_estimate=cost(7),
        name="project",
    )(power, images, sketch)


def gather_kernel(index_ref, table_ref, out_ref):
    docs = table_ref.shape[0]
    group, _, rows = index_ref.shape
    lane = lax.broadcasted_iota(jnp.int32, (rows, LANES), 1).astype(F32)
    hots = []
    for g in range(group):
        index = jnp.broadcast_to(index_ref[g].astype(F32), (LANES, rows)).T
        hots.append(
            jnp.concatenate(
                [jnp.where(index == lane + float(k), 1.0, 0.0).astype(BF16) for k in range(0, docs, LANES)],
                axis=1,
            )
        )
    found = jnp.dot(jnp.concatenate(hots, axis=0), table_ref[...], preferred_element_type=F32)
    out_ref[...] = found.astype(BF16).reshape(out_ref.shape)


def gather_rows(index, table):
    senders, rows = index.shape
    docs, columns = table.shape
    group = 4
    return pl.pallas_call(
        gather_kernel,
        grid=(senders // group,),
        in_specs=[
            pl.BlockSpec((group, 1, rows), lambda s: (s, 0, 0)),
            pl.BlockSpec((docs, columns), lambda s: (0, 0)),
        ],
        out_specs=pl.BlockSpec((group, rows, columns), lambda s: (s, 0, 0)),
        out_shape=jax.ShapeDtypeStruct((senders, rows, columns), BF16),
        compiler_params=params(58),
        cost_estimate=cost(3),
        name="gather_rows",
    )(index.reshape(senders, 1, rows), table)


def scale_kernel(block_ref, vals_ref, scale_ref, turned_ref, square_ref):
    square_ref[...] = jnp.zeros_like(square_ref)

    def slot(s, carry):
        weights = vals_ref[s].astype(F32)
        block = block_ref[s]
        square_ref[pl.ds(block, 1), :] += jnp.sum(weights * weights, axis=0, keepdims=True)
        turned_ref[s] = vals_ref[s].T
        return carry

    lax.fori_loop(0, vals_ref.shape[0], slot, 0)
    width = vals_ref.shape[2]
    for b in range(square_ref.shape[0]):
        root = lax.rsqrt(square_ref[b : b + 1, :] + 1.0)
        scale_ref[b * width : (b + 1) * width, :] = jnp.broadcast_to(root, (LANES, width)).T


def row_scales(blocks, vals):
    width = vals.shape[2]
    count = VOCAB_DEV // width
    return pl.pallas_call(
        scale_kernel,
        in_specs=[IN_SMEM, FULL_VMEM],
        out_specs=(FULL_VMEM, FULL_VMEM),
        out_shape=(
            jax.ShapeDtypeStruct((VOCAB_DEV, LANES), F32),
            jax.ShapeDtypeStruct((vals.shape[0], width, vals.shape[1]), BF16),
        ),
        scratch_shapes=[pltpu.VMEM((count, width), F32)],
        compiler_params=params(58),
        cost_estimate=cost(3),
        name="row_scales",
    )(blocks, vals)


def collect_kernel(earlier, sources, half_ref, block_ref, vals_hbm, scale_hbm, *refs):
    count = 2 * earlier
    rows_hbm, refs = refs[:sources], refs[sources:]
    before_hbm = refs[:count]
    high_ref, low_ref, gram_ref, sum_ref, vals_ref, scale_ref = refs[count : count + 6]
    rows_refs, refs = refs[count + 6 : count + 6 + sources], refs[count + 6 + sources :]
    before, arrivals = refs[:count], refs[count]
    slots, width, _ = vals_ref.shape
    columns = high_ref.shape[1]
    part = slots // sources
    half = half_ref[0]
    starts = [0] if sources == 1 else [half * part, (1 - half) * part]
    moves = []
    for i in range(sources):
        moves.append((vals_hbm.at[pl.ds(starts[i], part)], vals_ref.at[pl.ds(i * part, part)]))
        moves.append((rows_hbm[i], rows_refs[i]))
    moves.append((scale_hbm, scale_ref))
    moves += list(zip(before_hbm, before))
    copies = [pltpu.make_async_copy(src, dst, arrivals.at[i]) for i, (src, dst) in enumerate(moves)]
    for copy in copies:
        copy.start()
    sum_ref[...] = jnp.zeros_like(sum_ref)
    unroll = 8

    for i in range(sources):
        copies[2 * i].wait()
        copies[2 * i + 1].wait()

        def group(g, carry):
            parts = [
                jnp.dot(
                    vals_ref[i * part + g * unroll + u],
                    rows_refs[i][g * unroll + u],
                    preferred_element_type=F32,
                )
                for u in range(unroll)
            ]
            for u in range(unroll):
                at = pl.multiple_of(block_ref[starts[i] + g * unroll + u] * width, width)
                sum_ref[pl.ds(at, width), :] += parts[u]
            return carry

        lax.fori_loop(0, part // unroll, group, 0)
    for copy in copies[2 * sources :]:
        copy.wait()
    gram_ref[...] = jnp.zeros_like(gram_ref)
    step = 512

    def tile(t, carry):
        at = pl.ds(pl.multiple_of(t * step, step), step)
        scale = scale_ref[at, :]
        whole = sum_ref[at, :] * jnp.concatenate([scale] * (columns // LANES), axis=1)
        high, low = split2(whole)
        high_ref[at, :] = high
        low_ref[at, :] = low
        place = 0
        for e in range(earlier + 1):
            if e < earlier:
                other_high, other_low = before[2 * e][at, :], before[2 * e + 1][at, :]
            else:
                other_high, other_low = high, low
            wide = other_high.shape[1]
            gram_ref[:, place : place + wide] += (
                dot(high, other_high, 0, 0) + dot(low, other_high, 0, 0) + dot(high, other_low, 0, 0)
            )
            place += wide
        return carry

    lax.fori_loop(0, VOCAB_DEV // step, tile, 0)


def collect(half, blocks, vals, scales, rows, before):
    columns = rows[0].shape[2]
    known = sum(high.shape[1] for high, low in before)
    flat = [piece for pair in before for piece in pair]
    moved = len(rows) * 2 + 1 + len(flat)
    return pl.pallas_call(
        lambda *refs: collect_kernel(len(before), len(rows), *refs),
        in_specs=[IN_SMEM] * 2 + [IN_HBM] * (2 + len(rows) + len(flat)),
        out_specs=(FULL_VMEM,) * 3,
        out_shape=(
            jax.ShapeDtypeStruct((VOCAB_DEV, columns), BF16),
            jax.ShapeDtypeStruct((VOCAB_DEV, columns), BF16),
            jax.ShapeDtypeStruct((columns, known + columns), F32),
        ),
        scratch_shapes=[
            pltpu.VMEM((VOCAB_DEV, columns), F32),
            pltpu.VMEM(vals.shape, BF16),
            pltpu.VMEM(scales.shape, F32),
        ]
        + [pltpu.VMEM(piece.shape, BF16) for piece in list(rows) + flat]
        + [pltpu.SemaphoreType.DMA((moved,))],
        compiler_params=params(58),
        cost_estimate=cost(5),
        name="collect",
    )(half, blocks, vals, scales, *rows, *flat)


def factor_block(rest_ref, unit_ref, upper_ref, inverse_ref):
    size = rest_ref.shape[0]
    lane = lax.broadcasted_iota(jnp.int32, (8, size), 1)
    sub = lax.broadcasted_iota(jnp.int32, (8, size), 0)

    def spread(row):
        return jnp.broadcast_to(row, (8, size))

    def panel(p, carry):
        first = pl.multiple_of(p * 8, 8)
        rows = rest_ref[pl.ds(first, 8), :]
        inverse = unit_ref[pl.ds(first, 8), :]
        columns = [
            spread(jnp.sum(jnp.where(lane == first + j, rows, 0.0), axis=1, keepdims=True))
            for j in range(8)
        ]
        for j in range(8):
            root = lax.rsqrt(spread(columns[j][j : j + 1, :]))
            lower = columns[j] * root
            for m in range(j + 1, 8):
                columns[m] = columns[m] - lower * spread(lower[m : m + 1, :])
            below = jnp.where(sub > j, lower, 0.0)
            row = spread(rows[j : j + 1, :]) * root
            rows = jnp.where(sub == j, row, rows - below * row)
            row = spread(inverse[j : j + 1, :]) * root
            inverse = jnp.where(sub == j, row, inverse - below * row)
        rows = jnp.where(lane >= first + sub, rows, 0.0)
        upper_ref[pl.ds(first, 8), :] = rows
        inverse_ref[pl.ds(first, 8), :] = inverse
        a, b, c = split3(rows)
        x, y, z = split3(inverse)
        left = jnp.concatenate([a, a, b, a, c, b], axis=0).T.astype(BF16)
        right = jnp.concatenate(
            [jnp.concatenate([a, b, a, c, a, b], axis=0), jnp.concatenate([x, y, x, z, x, y], axis=0)],
            axis=1,
        ).astype(BF16)
        update = jnp.dot(left, right, preferred_element_type=F32)
        rest_ref[...] -= update[:, :size]
        unit_ref[...] -= update[:, size:]
        return carry

    lax.fori_loop(0, size // 8, panel, 0)


def cholesky_kernel(row, root, last, count, gram_ref, *refs):
    refs = list(refs)
    size = LANES
    if count:
        known_ref = refs.pop(0)
    before = [refs.pop(0) for _ in range(count if last else 0)]
    inverse_ref, upper_ref, rest_ref, unit_ref, piece_ref, small_ref = refs
    known = count * size
    mine = slice(row * size, (row + 1) * size)
    corner = gram_ref[mine, known : known + size]
    if count:
        left = exact(gram_ref[mine, :known], known_ref[...], 1, 1)
        corner = corner - exact(left, left, 1, 1)
    rest_ref[...] = corner
    square = (size, size)
    unit_ref[...] = jnp.where(
        lax.broadcasted_iota(jnp.int32, square, 0) == lax.broadcasted_iota(jnp.int32, square, 1), 1.0, 0.0
    )
    factor_block(rest_ref, unit_ref, piece_ref, small_ref)
    small = small_ref[...]
    place = known if last else 0
    if last:
        upper_ref[...] = jnp.zeros_like(upper_ref)
        for e in range(count):
            upper_ref[: (e + 1) * size, e * size : (e + 1) * size] = before[e][...]
    if count:
        inverse_ref[:known, :known] = known_ref[...]
        inverse_ref[:known, known:] = jnp.zeros((known, size), F32)
        inverse_ref[known:, :known] = -exact(small, exact(left, known_ref[...], 1, 0), 1, 0)
        upper_ref[:known, place : place + size] = left.T * (1.0 / root)
    inverse_ref[known:, known:] = small
    upper_ref[known:, place : place + size] = piece_ref[...] * (1.0 / root)


def cholesky_step(gram, row, inverse, before, root, last):
    count = len(before)
    total = (count + 1) * LANES
    inputs = [gram] + ([inverse] if count else []) + (list(before) if last else [])
    square = pltpu.VMEM((LANES, LANES), F32)
    return pl.pallas_call(
        lambda *refs: cholesky_kernel(row, root, last, count, *refs),
        in_specs=[FULL_VMEM] * len(inputs),
        out_specs=(FULL_VMEM,) * 2,
        out_shape=(
            jax.ShapeDtypeStruct((total, total), F32),
            jax.ShapeDtypeStruct((total, total if last else LANES), F32),
        ),
        scratch_shapes=[square] * 4,
        compiler_params=params(16),
        cost_estimate=cost(8),
        name="cholesky_step",
    )(*inputs)


def basis_kernel(pieces, known, root, inverse_ref, *refs):
    out_ref = refs[-1]
    total = None
    place = 0
    for e in range(pieces):
        high, low = refs[2 * e][...], refs[2 * e + 1][...]
        wide = high.shape[1]
        part_high, part_low = split2(inverse_ref[known:, place : place + wide])
        term = dot(high, part_high, 1, 1) + dot(low, part_high, 1, 1) + dot(high, part_low, 1, 1)
        total = term if total is None else total + term
        place += wide
    out_ref[...] = total * root


def basis_block(inverse, pieces, buffer, root, columns_total):
    columns = pieces[-1][0].shape[1]
    total = inverse.shape[0]
    known = total - columns
    step = 512
    flat = [piece for pair in pieces for piece in pair]
    in_specs = [pl.BlockSpec((total, total), lambda t: (0, 0))]
    in_specs += [pl.BlockSpec((step, piece.shape[1]), lambda t: (t, 0)) for piece in flat]
    inputs = [inverse] + flat
    aliases = {}
    if buffer is not None:
        aliases = {len(inputs): 0}
        inputs.append(buffer)
        in_specs.append(pl.BlockSpec(memory_space=pl.ANY))
    return pl.pallas_call(
        lambda *refs: basis_kernel(len(pieces), known, root, *refs),
        grid=(VOCAB_DEV // step,),
        in_specs=in_specs,
        out_specs=pl.BlockSpec((step, columns), lambda t: (t, known // columns)),
        out_shape=jax.ShapeDtypeStruct((VOCAB_DEV, columns_total), F32),
        input_output_aliases=aliases,
        compiler_params=params(58),
        cost_estimate=cost(3),
        name="basis_block",
    )(*inputs)


def swap(x, axis, bit):
    size = lax.axis_size(axis)
    return lax.ppermute(x, axis, [(i, i ^ bit) for i in range(size)])


def bits(axis):
    size = lax.axis_size(axis)
    return [1 << k for k in range(size.bit_length() - 1)]


def sum_all(x):
    for axis in ("docs", "rest", "half"):
        for bit in bits(axis):
            x = x + swap(x, axis, bit)
    return x


def sum_halves(x):
    half = x.shape[0] // 2
    odd = lax.axis_index("docs") % 2
    mine = lax.dynamic_slice_in_dim(x, odd * half, half)
    other = lax.dynamic_slice_in_dim(x, (1 - odd) * half, half)
    mine = mine + swap(other, "docs", 1)
    for axis in ("docs", "rest", "half"):
        for bit in bits(axis):
            if axis != "docs" or bit > 1:
                mine = mine + swap(mine, axis, bit)
    other = swap(mine, "docs", 1)
    return jnp.concatenate(
        [jnp.where(odd == 0, mine, other), jnp.where(odd == 0, other, mine)], axis=0
    )


def body(images, sketch, tile_vals, tile_rows, tile_count, tile_block):
    side = lax.axis_size("rest") * lax.axis_size("docs")
    senders = 2 * side
    doc_rows = images.shape[0]
    capacity, tile_height, tile_width = tile_vals.shape[2:]
    columns = sketch.shape[1]
    slots = senders * capacity
    cut = FIRST_PART * LANES
    half = lax.axis_index("half")
    outgoing, power = prepare(tile_count, images, tile_vals)
    vals = lax.all_to_all(
        outgoing.reshape(senders, capacity * tile_height, tile_width), BOTH, 0, 0, tiled=True
    )
    vals = vals.reshape(slots, tile_height, tile_width)
    power = sum_all(power)
    index = tile_rows[0].reshape(senders, capacity * tile_height)
    halves = index.reshape(2, side, capacity * tile_height)
    near_index = lax.dynamic_index_in_dim(halves, half, 0, keepdims=False)
    far_index = swap(lax.dynamic_index_in_dim(halves, 1 - half, 0, keepdims=False), "half", 1)
    blocks = tile_block[0].reshape(slots)
    root = math.sqrt(VOCAB_DEV * senders)
    scale, turned = row_scales(blocks, vals)
    where = half.reshape(1).astype(jnp.int32)
    table, last_table = project(power, images, sketch, doc_rows * senders, cut)
    far_table = swap(table, "half", 1)
    near = gather_rows(near_index, table)
    near = lax.all_to_all(near, SIDE, 0, 0, tiled=True)
    far = gather_rows(far_index, far_table)
    far = lax.all_to_all(far, SIDE, 0, 0, tiled=True)
    final = gather_rows(index, last_table)
    final = lax.all_to_all(final, BOTH, 0, 0, tiled=True)

    def by_slot(rows):
        return rows.reshape(-1, tile_height, rows.shape[2])

    pieces, uppers = [], []
    inverse = basis = None
    for rows in [[by_slot(near), by_slot(far)], [by_slot(final)]]:
        high, low, gram = collect(where, blocks, turned, scale, rows, pieces)
        pieces.append((high, low))
        gram = sum_halves(gram)
        for row in range(gram.shape[0] // LANES):
            last = (len(uppers) + 1) * LANES == columns
            inverse, upper = cholesky_step(gram, row, inverse, uppers, root, last)
            uppers.append(upper)
        basis = basis_block(inverse, pieces, basis, root, columns)
    return (basis, uppers[-1])


def solution(mesh):
    split = (2, mesh.shape["vocab"] // 2, mesh.shape["docs"])
    finer = jax.sharding.Mesh(mesh.devices.reshape(split), BOTH)
    placed = (
        P(BOTH, None),
        P(),
        P(BOTH, None, None, None, None),
        P(BOTH, None, None, None),
        P(BOTH, None),
        P(BOTH, None, None),
    )
    return jax.shard_map(
        body,
        mesh=finer,
        in_specs=placed,
        out_specs=(P(BOTH, None), P()),
        check_vma=False,
    )
```

time: 553 us -> 258 us (0.47); the launches traced: 546 us -> 257 us
  other arithmetic: 136 us -> 2.94 us
  waiting for transfers between devices: 224 us -> 102 us
  Pallas kernels: 0 us -> 99 us
  matrix products: 78.2 us -> 0 us
  blocking collectives: 41.3 us -> 0 us
  starting transfers between devices: 12.2 us -> 43.2 us
  local copies, waits for them, and re-layouts: 36.8 us -> 8.83 us
  between operations: 17.1 us -> 0.94 us
    psum x1 -> x0, waiting for transfers between devices: 130 us -> none  [body(): lax.psum(jnp.dot(sketch_rows.T, sketch_rows, precision=lax.Precision.HIGH...]
    another operation x16 -> x0, other arithmetic: 119 us -> none  [the longest x14 78.8 us: body(): lower_first = jnp.linalg.cholesky(gram_first)]
    pallas_call x0 -> x14, Pallas kernels: none -> 99 us  [the longest x4 30.6 us: cholesky_step(): pl.pallas_call(lambda *refs: cholesky_kernel(row, root, last, count, *ref...]
    ppermute x0 -> x19, waiting for transfers between devices: none -> 83.8 us  [swap(): return lax.ppermute(x, axis, [(i, i ^ bit) for i in range(size)])]
    all_to_all x2 -> x4, waiting for transfers between devices: 93.1 us -> 18 us  [the longest x1 15.4 us: body(): far = lax.all_to_all(far, SIDE, 0, 0, tiled=True)]
    dot_general x8 -> x0, matrix products: 58.6 us -> none  [the longest x2 28.3 us: collect(): jnp.einsum('sb,skj->bkj', slot_hot, product, precision=lax.Precision.HIGH...]
    psum x1 -> x0, blocking collectives: 41.3 us -> none  [body(): feature_sums = lax.psum(feature_sums, ('vocab', 'docs'))]
    ppermute x0 -> x19, starting transfers between devices: none -> 23.3 us  [swap(): return lax.ppermute(x, axis, [(i, i ^ bit) for i in range(size)])]
  transfers between devices with their start and end apart: 3 -> 23, of which waited for: 2 -> 16; matrix products, arithmetic and copies ran while one was open for 6% -> 3% of each run, Pallas kernels for 0% -> 20%
where the time goes in v1:
time: 258 us; the launch traced here: 257 us
  waiting for transfers between devices  102 us (40%)
  Pallas kernels  99 us (38%)
  starting transfers between devices  43.2 us (17%)
  local copies, waits for them, and re-layouts  8.83 us (3%)
  other arithmetic  2.94 us (1%)
    ppermute x19, waiting for transfers between devices, swap(): return lax.ppermute(x, axis, [(i, i ^ bit) for i in range(size)])  83.8 us
    pallas_call x4, Pallas kernels, cholesky_step(): pl.pallas_call(lambda *refs: cholesky_kernel(row, root, last, count, *ref...  30.6 us
    ppermute x19, starting transfers between devices, swap(): return lax.ppermute(x, axis, [(i, i ^ bit) for i in range(size)])  23.3 us
    pallas_call x2, Pallas kernels, collect(): pl.pallas_call(lambda *refs: collect_kernel(len(before), len(rows), *refs...  17 us
    pallas_call x3, Pallas kernels, gather_rows(): pl.pallas_call(gather_kernel, grid=(senders // group,), in_specs=[pl.Bloc...  16.4 us
    all_to_all x1, waiting for transfers between devices, body(): far = lax.all_to_all(far, SIDE, 0, 0, tiled=True)  15.4 us
    pallas_call x2, Pallas kernels, basis_block(): pl.pallas_call(lambda *refs: basis_kernel(len(pieces), known, root, *refs...  12.1 us
    pallas_call x1, Pallas kernels, project(): pl.pallas_call(lambda *refs: project_kernel(documents, steps, *refs), in_...  9.61 us
  transfers between devices with their start and end apart: 23, of which 16 were waited for; matrix products, arithmetic and copies ran while one was open for 3% of the time, Pallas kernels for 20%

profile of v1, /device:TPU:0, one launch (start us, length us, event | category | flops | bytes accessed | tf_op | source)
XLA Modules:
  0.0 256.7 jit_solution(11833451426582493176)
XLA Ops:
  0.6 5.8 %prepare.1 = (bf16[32,2,64,128]{3,2,1,0:T(8,128)(2,1)}, f32[1,4096]{1,0:T(1,128)}) custom-call(s32[1,32]{1,0:T(1,128)} %refs_0_.1, bf16[1024,4096]{1,0:T(8,128)(2,1)} %refs_1_.3, bf16[1,32,2,64,128]{4,3,2,1,0:T(8,128)(2,1)} %refs_2_.2), custom_call_target="tpu_custom_call" | custom-call | flops 4000000000 | tf_op jit(solution)/shard_map/prepare/pallas_call | solution.py:92
  6.4 7.3 %all-to-all-start = ((bf16[32,128,128]{2,1,0:T(8,128)(2,1)}), bf16[32,128,128]{2,1,0:T(8,128)(2,1)S(1)}, u32[]{:S(2)}, u32[]{:S(2)}) async-start(bf16[32,128,128]{2,1,0:T(8,128)(2,1)} %bitcast.14), calls=%async_computation | async-start | bytes 2097152 | tf_op jit(solution)/shard_map/all_to_all | solution.py:518
  16.9 4.9 %collective-permute-done.1 = f32[1,4096]{1,0:T(1,128)S(1)} collective-permute-done((f32[1,4096]{1,0:T(1,128)S(1)}, f32[1,4096]{1,0:T(1,128)S(1)}, u32[]{:S(2)}, u32[]{:S(2)}) %collective-permute-start.1) | collective-permute-done | bytes 16416 | tf_op jit(solution)/shard_map/ppermute | solution.py:477
  27.0 4.8 %collective-permute-done.3 = f32[1,4096]{1,0:T(1,128)S(1)} collective-permute-done((f32[1,4096]{1,0:T(1,128)S(1)}, f32[1,4096]{1,0:T(1,128)S(1)}, u32[]{:S(2)}, u32[]{:S(2)}) %collective-permute-start.3) | collective-permute-done | bytes 16416 | tf_op jit(solution)/shard_map/ppermute | solution.py:477
  31.8 4.5 %collective-permute-start.4 = (f32[1,4096]{1,0:T(1,128)S(1)}, f32[1,4096]{1,0:T(1,128)S(1)}, u32[]{:S(2)}, u32[]{:S(2)}) collective-permute-start(f32[1,4096]{1,0:T(1,128)S(1)} %add.74), channel_id=1, source_target_pairs={{0,16},{16,0},{1,17},{17,1},{2,18},{18,2},{3,19},{19,3},{4,20},{20... | collective-permute-start | bytes 49160 | tf_op jit(solution)/shard_map/ppermute | solution.py:477
  41.3 9.6 %project.1 = (bf16[1024,384]{1,0:T(8,128)(2,1)}, bf16[1024,128]{1,0:T(8,128)(2,1)}) custom-call(f32[1,4096]{1,0:T(1,128)} %add.75.refs_0_, bf16[1024,4096]{1,0:T(8,128)(2,1)} %refs_1_.3, bf16[4096,512]{1,0:T(8,128)(2,1)} %refs_2_.3), custom_call_target="tpu_custom_call" | custom-call | flops 7000000000 | tf_op jit(solution)/shard_map/project/pallas_call | solution.py:147
  50.9 5.0 %gather_rows.4 = bf16[16,128,384]{2,1,0:T(8,128)(2,1)} custom-call(s32[16,1,128]{2,1,0:T(1,128)} %bitcast.15, bf16[1024,384]{1,0:T(8,128)(2,1)} %get-tuple-element.27.table_ref), custom_call_target="tpu_custom_call" | custom-call | flops 3000000000 | tf_op jit(solution)/shard_map/gather_rows/pallas_call | solution.py:188
  62.7 35.2 %collective-permute-done.5 = s32[16,128]{1,0:T(8,128)S(1)} collective-permute-done((s32[16,128]{1,0:T(8,128)S(1)}, s32[16,128]{1,0:T(8,128)S(1)}, u32[]{:S(2)}, u32[]{:S(2)}) %collective-permute-start.5) | collective-permute-done | bytes 8224 | tf_op jit(solution)/shard_map/ppermute | solution.py:477
  98.8 5.0 %gather_rows.5 = bf16[16,128,384]{2,1,0:T(8,128)(2,1)} custom-call(s32[16,1,128]{2,1,0:T(1,128)} %bitcast.16, bf16[1024,384]{1,0:T(8,128)(2,1)} %copy-done.10), custom_call_target="tpu_custom_call" | custom-call | flops 3000000000 | tf_op jit(solution)/shard_map/gather_rows/pallas_call | solution.py:188
  105.0 4.1 %all-to-all-start.3 = ((bf16[16,128,384]{2,1,0:T(8,128)(2,1)}), bf16[16,128,384]{2,1,0:T(8,128)(2,1)S(1)}, u32[]{:S(2)}, u32[]{:S(2)}) async-start(bf16[16,128,384]{2,1,0:T(8,128)(2,1)} %gather_rows.5), calls=%async_computation.3 | async-start | bytes 3145728 | tf_op jit(solution)/shard_map/all_to_all | solution.py:536
  109.8 6.4 %gather_rows.3 = bf16[32,128,128]{2,1,0:T(8,128)(2,1)} custom-call(s32[32,1,128]{2,1,0:T(1,128)} %reshape_reshape_squeeze.6.index_ref, bf16[1024,128]{1,0:T(8,128)(2,1)} %get-tuple-element.26.table_ref), custom_call_target="tpu_custom_call" | custom-call | flops 3000000000 | tf_op jit(solution)/shard_map/gather_rows/pallas_call | solution.py:188
  116.2 15.4 %all-to-all-done.3 = bf16[16,128,384]{2,1,0:T(8,128)(2,1)S(1)} async-done(((bf16[16,128,384]{2,1,0:T(8,128)(2,1)}), bf16[16,128,384]{2,1,0:T(8,128)(2,1)S(1)}, u32[]{:S(2)}, u32[]{:S(2)}) %all-to-all-start.3) | async-done | bytes 1572896 | tf_op jit(solution)/shard_map/all_to_all | solution.py:536
  131.6 4.7 %all-to-all-start.1 = ((bf16[32,128,128]{2,1,0:T(8,128)(2,1)}), bf16[32,128,128]{2,1,0:T(8,128)(2,1)S(1)}, u32[]{:S(2)}, u32[]{:S(2)}) async-start(bf16[32,128,128]{2,1,0:T(8,128)(2,1)} %gather_rows.3), calls=%async_computation.1 | async-start | bytes 2097152 | tf_op jit(solution)/shard_map/all_to_all | solution.py:538
  137.0 7.5 %row_scales.1 = (f32[2048,128]{1,0:T(8,128)}, bf16[64,128,64]{2,1,0:T(8,128)(2,1)}) custom-call(s32[64]{0:T(128)} %reshape_squeeze.3.block_ref.refs_1_, bf16[64,64,128]{2,1,0:T(8,128)(2,1)} %bitcast.12), custom_call_target="tpu_custom_call" | custom-call | flops 3000000000 | tf_op jit(solution)/shard_map/row_scales/pallas_call | solution.py:223
  144.5 9.9 %collect.2 = (bf16[2048,384]{1,0:T(8,128)(2,1)}, bf16[2048,384]{1,0:T(8,128)(2,1)}, f32[384,384]{1,0:T(8,128)}) custom-call(s32[1]{0:T(128)} %bitcast.refs_0_, s32[64]{0:T(128)} %reshape_squeeze.3.block_ref.refs_1_, bf16[64,128,64]{2,1,0:T(8,128)(2,1)} %get-tuple-element.23.refs_2_, f32[2048,128]{1,0:T(8,128)} %get-tuple-element.24.refs_3_, ...), custom_call_target="tpu_custom_call" | custom-call | flops 5000000000 | tf_op jit(solution)/shard_map/collect/pallas_call | solution.py:314
  163.3 7.1 %collect.3 = (bf16[2048,128]{1,0:T(8,128)(2,1)}, bf16[2048,128]{1,0:T(8,128)(2,1)}, f32[128,512]{1,0:T(8,128)}) custom-call(s32[1]{0:T(128)} %bitcast.refs_0_, s32[64]{0:T(128)} %reshape_squeeze.3.block_ref.refs_1_, bf16[64,128,64]{2,1,0:T(8,128)(2,1)} %get-tuple-element.23.refs_2_, f32[2048,128]{1,0:T(8,128)} %get-tuple-element.24.refs_3_, ...), custom_call_target="tpu_custom_call" | custom-call | flops 5000000000 | tf_op jit(solution)/shard_map/collect/pallas_call | solution.py:314
  175.5 5.4 %collective-permute-done.15 = f32[192,384]{1,0:T(8,128)S(1)} collective-permute-done((f32[192,384]{1,0:T(8,128)S(1)}, f32[192,384]{1,0:T(8,128)S(1)}, u32[]{:S(2)}, u32[]{:S(2)}) %collective-permute-start.15) | collective-permute-done | bytes 294944 | tf_op jit(solution)/shard_map/ppermute | solution.py:477
  194.0 16.1 %collective-permute-done.11 = f32[64,512]{1,0:T(8,128)S(1)} collective-permute-done((f32[64,512]{1,0:T(8,128)S(1)}, f32[64,512]{1,0:T(8,128)S(1)}, u32[]{:S(2)}, u32[]{:S(2)}) %collective-permute-start.11) | collective-permute-done | bytes 131104 | tf_op jit(solution)/shard_map/ppermute | solution.py:477
  212.2 6.2 %cholesky_step.4 = (f32[128,128]{1,0:T(8,128)S(1)}, f32[128,128]{1,0:T(8,128)S(1)}) custom-call(f32[384,384]{1,0:T(8,128)S(1)} %pad_maximum_fusion.refs_0_), custom_call_target="tpu_custom_call" | custom-call | flops 8000000000 | tf_op jit(solution)/shard_map/cholesky_step/pallas_call | solution.py:419
  218.4 7.3 %cholesky_step.5 = (f32[256,256]{1,0:T(8,128)S(1)}, f32[256,128]{1,0:T(8,128)S(1)}) custom-call(f32[384,384]{1,0:T(8,128)S(1)} %pad_maximum_fusion.refs_0_, f32[128,128]{1,0:T(8,128)S(1)} %get-tuple-element.32.refs_1_), custom_call_target="tpu_custom_call" | custom-call | flops 8000000000 | tf_op jit(solution)/shard_map/cholesky_step/pallas_call | solution.py:419
  225.8 7.7 %cholesky_step.6 = (f32[384,384]{1,0:T(8,128)S(1)}, f32[384,128]{1,0:T(8,128)S(1)}) custom-call(f32[384,384]{1,0:T(8,128)S(1)} %pad_maximum_fusion.refs_0_, f32[256,256]{1,0:T(8,128)S(1)} %get-tuple-element.33.refs_1_), custom_call_target="tpu_custom_call" | custom-call | flops 8000000000 | tf_op jit(solution)/shard_map/cholesky_step/pallas_call | solution.py:419
  234.3 6.5 %basis_block.2.refs_5_ = f32[2048,512]{1,0:T(8,128)} custom-call(f32[384,384]{1,0:T(8,128)} %copy-done.1, bf16[2048,384]{1,0:T(8,128)(2,1)} %get-tuple-element.28.refs_5_.refs_1_, bf16[2048,384]{1,0:T(8,128)(2,1)} %get-tuple-element.29.refs_6_.refs_2_), custom_call_target="tpu_custom_call" | custom-call | flops 3000000000 | tf_op jit(solution)/shard_map/basis_block/pallas_call | solution.py:462
  240.8 9.3 %cholesky_step.7 = (f32[512,512]{1,0:T(8,128)S(1)}, f32[512,512]{1,0:T(8,128)}) custom-call(f32[128,512]{1,0:T(8,128)S(1)} %pad_maximum_fusion.1.refs_0_, f32[384,384]{1,0:T(8,128)S(1)} %copy-done.2, f32[128,128]{1,0:T(8,128)S(1)} %get-tuple-element.35.refs_2_, f32[256,128]{1,0:T(8,128)S(1)} %get-tuple-element.36.refs_3_, ...), custom_call_target="tpu_custom_call" | custom-call | flops 8000000000 | tf_op jit(solution)/shard_map/cholesky_step/pallas_call | solution.py:419
  251.1 5.6 %basis_block.3 = f32[2048,512]{1,0:T(8,128)} custom-call(f32[512,512]{1,0:T(8,128)} %copy-done, bf16[2048,384]{1,0:T(8,128)(2,1)} %get-tuple-element.28.refs_5_.refs_1_, bf16[2048,384]{1,0:T(8,128)(2,1)} %get-tuple-element.29.refs_6_.refs_2_, bf16[2048,128]{1,0:T(8,128)(2,1)} %get-tuple-element.39.refs_3_, ...), custom_call_target="tpu_custom_call", output_to_operand_aliasing={{}: (5, {})} | custom-call | flops 3000000000 | tf_op jit(solution)/shard_map/basis_block/pallas_call | solution.py:462
  (86 shorter events, 54.3 us)
Async XLA Ops:
  6.4 20.5 %copy-start.7 = (s32[1,32,2,64]{3,2,1,0:T(2,128)S(1)}, s32[1,32,2,64]{3,2,1,0:T(2,128)}, u32[]{:S(2)}) copy-start(s32[1,32,2,64]{3,2,1,0:T(2,128)} %param.9) | copy-start | bytes 49156
  6.4 49.5 %all-to-all-start = ((bf16[32,128,128]{2,1,0:T(8,128)(2,1)}), bf16[32,128,128]{2,1,0:T(8,128)(2,1)S(1)}, u32[]{:S(2)}, u32[]{:S(2)}) async-start(bf16[32,128,128]{2,1,0:T(8,128)(2,1)} %bitcast.14), calls=%async_computation | async-start | bytes 2097152 | tf_op jit(solution)/shard_map/all_to_all | solution.py:518
  13.8 1.2 collective-permute-start
  15.1 6.7 %collective-permute-start.1 = (f32[1,4096]{1,0:T(1,128)S(1)}, f32[1,4096]{1,0:T(1,128)S(1)}, u32[]{:S(2)}, u32[]{:S(2)}) collective-permute-start(f32[1,4096]{1,0:T(1,128)S(1)} %add.71), channel_id=1, source_target_pairs={{0,2},{1,3},{2,0},{3,1},{4,6},{5,7},{6,4},{7,5},{8,10},{9,11},{10,... | collective-permute-start | bytes 49160 | tf_op jit(solution)/shard_map/ppermute | solution.py:477
  21.8 4.6 %collective-permute-start.2 = (f32[1,4096]{1,0:T(1,128)S(1)}, f32[1,4096]{1,0:T(1,128)S(1)}, u32[]{:S(2)}, u32[]{:S(2)}) collective-permute-start(f32[1,4096]{1,0:T(1,128)S(1)} %add.72), channel_id=1, source_target_pairs={{0,4},{4,0},{8,12},{12,8},{1,5},{5,1},{9,13},{13,9},{2,6},{6,2},{1... | collective-permute-start | bytes 49160 | tf_op jit(solution)/shard_map/ppermute | solution.py:477
  26.5 5.3 %collective-permute-start.3 = (f32[1,4096]{1,0:T(1,128)S(1)}, f32[1,4096]{1,0:T(1,128)S(1)}, u32[]{:S(2)}, u32[]{:S(2)}) collective-permute-start(f32[1,4096]{1,0:T(1,128)S(1)} %add.73), channel_id=1, source_target_pairs={{0,8},{4,12},{8,0},{12,4},{1,9},{5,13},{9,1},{13,5},{2,10},{6,14},... | collective-permute-start | bytes 49160 | tf_op jit(solution)/shard_map/ppermute | solution.py:477
  31.8 8.9 %collective-permute-start.4 = (f32[1,4096]{1,0:T(1,128)S(1)}, f32[1,4096]{1,0:T(1,128)S(1)}, u32[]{:S(2)}, u32[]{:S(2)}) collective-permute-start(f32[1,4096]{1,0:T(1,128)S(1)} %add.74), channel_id=1, source_target_pairs={{0,16},{16,0},{1,17},{17,1},{2,18},{18,2},{3,19},{19,3},{4,20},{20... | collective-permute-start | bytes 49160 | tf_op jit(solution)/shard_map/ppermute | solution.py:477
  55.9 47.9 %all-to-all-start.2 = ((bf16[16,128,384]{2,1,0:T(8,128)(2,1)}), bf16[16,128,384]{2,1,0:T(8,128)(2,1)S(1)}, u32[]{:S(2)}, u32[]{:S(2)}) async-start(bf16[16,128,384]{2,1,0:T(8,128)(2,1)} %gather_rows.4), calls=%async_computation.2 | async-start | bytes 3145728 | tf_op jit(solution)/shard_map/all_to_all | solution.py:534
  59.7 38.2 %collective-permute-start.6 = (bf16[1024,384]{1,0:T(8,128)(2,1)}, bf16[1024,384]{1,0:T(8,128)(2,1)S(1)}, u32[]{:S(2)}, u32[]{:S(2)}) collective-permute-start(bf16[1024,384]{1,0:T(8,128)(2,1)} %get-tuple-element.27.table_ref), channel_id=1, source_target_pairs={{0,16},{16,0},{1,17},{17,1},{2,18},{18,2},{3,19},{19,3},{4,20},{20... | collective-permute-start | bytes 2359304 | tf_op jit(solution)/shard_map/ppermute | solution.py:477
  61.2 36.7 %collective-permute-start.5 = (s32[16,128]{1,0:T(8,128)S(1)}, s32[16,128]{1,0:T(8,128)S(1)}, u32[]{:S(2)}, u32[]{:S(2)}) collective-permute-start(s32[16,128]{1,0:T(8,128)S(1)} %get-tuple-element.46), channel_id=1, source_target_pairs={{0,16},{16,0},{1,17},{17,1},{2,18},{18,2},{3,19},{19,3},{4,20},{20... | collective-permute-start | bytes 24584 | tf_op jit(solution)/shard_map/ppermute | solution.py:477
  105.0 26.6 %all-to-all-start.3 = ((bf16[16,128,384]{2,1,0:T(8,128)(2,1)}), bf16[16,128,384]{2,1,0:T(8,128)(2,1)S(1)}, u32[]{:S(2)}, u32[]{:S(2)}) async-start(bf16[16,128,384]{2,1,0:T(8,128)(2,1)} %gather_rows.5), calls=%async_computation.3 | async-start | bytes 3145728 | tf_op jit(solution)/shard_map/all_to_all | solution.py:536
  131.6 30.7 %all-to-all-start.1 = ((bf16[32,128,128]{2,1,0:T(8,128)(2,1)}), bf16[32,128,128]{2,1,0:T(8,128)(2,1)S(1)}, u32[]{:S(2)}, u32[]{:S(2)}) async-start(bf16[32,128,128]{2,1,0:T(8,128)(2,1)} %gather_rows.3), calls=%async_computation.1 | async-start | bytes 2097152 | tf_op jit(solution)/shard_map/all_to_all | solution.py:538
  155.4 1.6 collective-permute-start.13
  158.0 13.4 %collective-permute-start.14 = (f32[192,384]{1,0:T(8,128)S(1)}, f32[192,384]{1,0:T(8,128)S(1)}, u32[]{:S(2)}, u32[]{:S(2)}) collective-permute-start(f32[192,384]{1,0:T(8,128)S(1)} %dynamic-slice_add_fusion), channel_id=1, source_target_pairs={{0,2},{1,3},{2,0},{3,1},{4,6},{5,7},{6,4},{7,5},{8,10},{9,11},{10,... | collective-permute-start | bytes 884744 | tf_op jit(solution)/shard_map/ppermute | solution.py:477
  171.4 1.7 collective-permute-start.7
  171.5 9.5 %collective-permute-start.15 = (f32[192,384]{1,0:T(8,128)S(1)}, f32[192,384]{1,0:T(8,128)S(1)}, u32[]{:S(2)}, u32[]{:S(2)}) collective-permute-start(f32[192,384]{1,0:T(8,128)S(1)} %add.88), channel_id=1, source_target_pairs={{0,4},{4,0},{8,12},{12,8},{1,5},{5,1},{9,13},{13,9},{2,6},{6,2},{1... | collective-permute-start | bytes 884744 | tf_op jit(solution)/shard_map/ppermute | solution.py:477
  174.0 8.0 %collective-permute-start.8 = (f32[64,512]{1,0:T(8,128)S(1)}, f32[64,512]{1,0:T(8,128)S(1)}, u32[]{:S(2)}, u32[]{:S(2)}) collective-permute-start(f32[64,512]{1,0:T(8,128)S(1)} %dynamic-slice_add_fusion.1), channel_id=1, source_target_pairs={{0,2},{1,3},{2,0},{3,1},{4,6},{5,7},{6,4},{7,5},{8,10},{9,11},{10,... | collective-permute-start | bytes 393224 | tf_op jit(solution)/shard_map/ppermute | solution.py:477
  181.0 9.9 %collective-permute-start.16 = (f32[192,384]{1,0:T(8,128)S(1)}, f32[192,384]{1,0:T(8,128)S(1)}, u32[]{:S(2)}, u32[]{:S(2)}) collective-permute-start(f32[192,384]{1,0:T(8,128)S(1)} %add.89), channel_id=1, source_target_pairs={{0,8},{4,12},{8,0},{12,4},{1,9},{5,13},{9,1},{13,5},{2,10},{6,14},... | collective-permute-start | bytes 884744 | tf_op jit(solution)/shard_map/ppermute | solution.py:477
  182.0 5.0 %collective-permute-start.9 = (f32[64,512]{1,0:T(8,128)S(1)}, f32[64,512]{1,0:T(8,128)S(1)}, u32[]{:S(2)}, u32[]{:S(2)}) collective-permute-start(f32[64,512]{1,0:T(8,128)S(1)} %add.81), channel_id=1, source_target_pairs={{0,4},{4,0},{8,12},{12,8},{1,5},{5,1},{9,13},{13,9},{2,6},{6,2},{1... | collective-permute-start | bytes 393224 | tf_op jit(solution)/shard_map/ppermute | solution.py:477
  187.0 6.0 %collective-permute-start.10 = (f32[64,512]{1,0:T(8,128)S(1)}, f32[64,512]{1,0:T(8,128)S(1)}, u32[]{:S(2)}, u32[]{:S(2)}) collective-permute-start(f32[64,512]{1,0:T(8,128)S(1)} %add.82), channel_id=1, source_target_pairs={{0,8},{4,12},{8,0},{12,4},{1,9},{5,13},{9,1},{13,5},{2,10},{6,14},... | collective-permute-start | bytes 393224 | tf_op jit(solution)/shard_map/ppermute | solution.py:477
  191.0 19.3 %collective-permute-start.17 = (f32[192,384]{1,0:T(8,128)S(1)}, f32[192,384]{1,0:T(8,128)S(1)}, u32[]{:S(2)}, u32[]{:S(2)}) collective-permute-start(f32[192,384]{1,0:T(8,128)S(1)} %add.90), channel_id=1, source_target_pairs={{0,16},{16,0},{1,17},{17,1},{2,18},{18,2},{3,19},{19,3},{4,20},{20... | collective-permute-start | bytes 884744 | tf_op jit(solution)/shard_map/ppermute | solution.py:477
  193.0 17.2 %collective-permute-start.11 = (f32[64,512]{1,0:T(8,128)S(1)}, f32[64,512]{1,0:T(8,128)S(1)}, u32[]{:S(2)}, u32[]{:S(2)}) collective-permute-start(f32[64,512]{1,0:T(8,128)S(1)} %add.83), channel_id=1, source_target_pairs={{0,16},{16,0},{1,17},{17,1},{2,18},{18,2},{3,19},{19,3},{4,20},{20... | collective-permute-start | bytes 393224 | tf_op jit(solution)/shard_map/ppermute | solution.py:477
  210.2 1.4 collective-permute-start.12
  210.4 1.8 collective-permute-start.18
  (11 other events, 57.5 us)

commit v2 on v1

--- a/solution.py
+++ b/solution.py
@@ -108,60 +108,109 @@
     )(count, images, vals)
 
 
-def project_kernel(
-    documents, steps, power_ref, images_hbm, sketch_hbm, first_ref, second_ref, images_ref, sketch_ref, scaled_ref, arrivals
-):
+def hot_rows(index, docs):
+    rows = index.shape[1]
+    spread = jnp.broadcast_to(index.astype(F32), (LANES, rows)).T
+    lane = lax.broadcasted_iota(jnp.int32, (rows, LANES), 1).astype(F32)
+    return jnp.concatenate(
+        [jnp.where(spread == lane + float(k), 1.0, 0.0).astype(BF16) for k in range(0, docs, LANES)], axis=1
+    )
+
+
+def project_kernel(documents, steps, group, power_ref, index_ref, images_hbm, sketch_hbm, *refs):
+    outputs = refs[:3]
+    images_ref, sketch_ref, scaled_ref, sum_ref, hot_ref, first_ref, second_ref, near_ref = refs[3:11]
+    arrivals, departures = refs[11:]
+    docs = images_ref.shape[1]
     features, columns = sketch_ref.shape
-    docs = images_ref.shape[0]
-    rows = docs // steps
     deep = features // steps
     copies = []
     for i in range(steps):
         at = pl.ds(i * deep, deep)
         copies.append(pltpu.make_async_copy(sketch_hbm.at[at], sketch_ref.at[at], arrivals.at[i]))
-    for i in range(steps):
-        at = pl.ds(i * rows, rows)
-        copies.append(pltpu.make_async_copy(images_hbm.at[at], images_ref.at[at], arrivals.at[steps + i]))
+        copies.append(pltpu.make_async_copy(images_hbm.at[:, at], images_ref.at[i], arrivals.at[steps + i]))
     for copy in copies:
         copy.start()
+    owners, _, rows = index_ref.shape
+
+    def build(o, carry):
+        hot_ref[pl.ds(pl.multiple_of(o * rows, rows), rows), :] = hot_rows(index_ref[o], docs)
+        return carry
+
+    lax.fori_loop(0, owners, build, 0)
+    cut = first_ref.shape[1]
     for i in range(steps):
-        copies[i].wait()
+        copies[2 * i].wait()
         for k in range(i * deep, (i + 1) * deep, LANES):
             scale = lax.rsqrt(power_ref[:, k : k + LANES] / documents + 1e-05)
             scale = jnp.broadcast_to(scale, (LANES, LANES)).T
             scale = jnp.concatenate([scale] * (columns // LANES), axis=1)
             scaled_ref[k : k + LANES, :] = (sketch_ref[k : k + LANES, :].astype(F32) * scale).astype(BF16)
-    cut = first_ref.shape[1]
-    for i in range(steps):
-        copies[steps + i].wait()
-        at = slice(i * rows, (i + 1) * rows)
-        found = jnp.dot(images_ref[at, :], scaled_ref[...], preferred_element_type=F32).astype(BF16)
-        first_ref[at, :] = found[:, :cut]
-        second_ref[at, :] = found[:, cut:]
-
-
-def project(power, images, sketch, documents, cut):
-    docs = images.shape[0]
-    _, columns = sketch.shape
-    steps = 4
-    return pl.pallas_call(
-        lambda *refs: project_kernel(documents, steps, *refs),
-        in_specs=[FULL_VMEM, IN_HBM, IN_HBM],
-        out_specs=(FULL_VMEM, FULL_VMEM),
-        out_shape=(
-            jax.ShapeDtypeStruct((docs, cut), BF16),
-            jax.ShapeDtypeStruct((docs, columns - cut), BF16),
-        ),
+        copies[2 * i + 1].wait()
+        for r in range(0, docs, docs // 2):
+            at = slice(r, r + docs // 2)
+            part = jnp.dot(
+                images_ref[i, at, :], scaled_ref[i * deep : (i + 1) * deep, :], preferred_element_type=F32
+            )
+            if i:
+                part = sum_ref[at, :] + part
+            if i < steps - 1:
+                sum_ref[at, :] = part
+            else:
+                found = part.astype(BF16)
+                first_ref[at, :] = found[:, :cut]
+                second_ref[at, :] = found[:, cut:]
+    sent = [
+        pltpu.make_async_copy(first_ref, outputs[0], departures.at[0]),
+        pltpu.make_async_copy(second_ref, outputs[1], departures.at[1]),
+    ]
+    for copy in sent:
+        copy.start()
+    for g in range(owners // group):
+        hot = hot_ref[g * group * rows : (g + 1) * group * rows, :]
+        found = jnp.dot(hot, first_ref[...], preferred_element_type=F32).astype(BF16)
+        at = slice(g * group, (g + 1) * group)
+        near_ref[at] = found.reshape(group, rows, cut)
+        copy = pltpu.make_async_copy(
+            near_ref.at[pl.ds(g * group, group)], outputs[2].at[pl.ds(g * group, group)], departures.at[2 + g]
+        )
+        copy.start()
+        sent.append(copy)
+    for copy in sent:
+        copy.wait()
+
+
+def project(power, index, images, sketch, documents, cut):
+    docs, features = images.shape
+    columns = sketch.shape[1]
+    owners, rows = index.shape
+    steps, group = 4, 4
+    shapes = [
+        jax.ShapeDtypeStruct((docs, cut), BF16),
+        jax.ShapeDtypeStruct((docs, columns - cut), BF16),
+        jax.ShapeDtypeStruct((owners, rows, cut), BF16),
+    ]
+    return pl.pallas_call(
+        lambda *refs: project_kernel(documents, steps, group, *refs),
+        in_specs=[FULL_VMEM, FULL_VMEM, IN_HBM, IN_HBM],
+        out_specs=(IN_HBM,) * 3,
+        out_shape=tuple(shapes),
         scratch_shapes=[
-            pltpu.VMEM(images.shape, BF16),
+            pltpu.VMEM((steps, docs, features // steps), BF16),
             pltpu.VMEM(sketch.shape, BF16),
             pltpu.VMEM(sketch.shape, BF16),
+            pltpu.VMEM((docs, columns), F32),
+            pltpu.VMEM((owners * rows, docs), BF16),
+        ]
+        + [pltpu.VMEM(shape.shape, BF16) for shape in shapes]
+        + [
             pltpu.SemaphoreType.DMA((2 * steps,)),
+            pltpu.SemaphoreType.DMA((2 + owners // group,)),
         ],
         compiler_params=params(58),
-        cost_estimate=cost(7),
+        cost_estimate=cost(9),
         name="project",
-    )(power, images, sketch)
+    )(power, index.reshape(owners, 1, rows), images, sketch)
 
 
 def gather_kernel(index_ref, table_ref, out_ref):
@@ -235,58 +284,77 @@
     )(blocks, vals)
 
 
-def collect_kernel(earlier, sources, half_ref, block_ref, vals_hbm, scale_hbm, *refs):
+def add_products(total_ref, vals_ref, rows_ref, block_ref, first_val, first_block, unroll):
+    width = vals_ref.shape[1]
+
+    def group(g, carry):
+        parts = [
+            jnp.dot(
+                vals_ref[first_val + g * unroll + u],
+                rows_ref[g * unroll + u],
+                preferred_element_type=F32,
+            )
+            for u in range(unroll)
+        ]
+        for u in range(unroll):
+            at = pl.multiple_of(block_ref[first_block + g * unroll + u] * width, width)
+            total_ref[pl.ds(at, width), :] += parts[u]
+        return carry
+
+    lax.fori_loop(0, rows_ref.shape[0] // unroll, group, 0)
+
+
+def begin_kernel(half_ref, block_ref, vals_ref, rows_ref, total_ref):
+    total_ref[...] = jnp.zeros_like(total_ref)
+    first = half_ref[0] * rows_ref.shape[0]
+    add_products(total_ref, vals_ref, rows_ref, block_ref, first, first, 8)
+
+
+def begin(half, blocks, vals, rows):
+    return pl.pallas_call(
+        begin_kernel,
+        in_specs=[IN_SMEM] * 2 + [FULL_VMEM] * 2,
+        out_specs=FULL_VMEM,
+        out_shape=jax.ShapeDtypeStruct((VOCAB_DEV, rows.shape[2]), F32),
+        compiler_params=params(58),
+        cost_estimate=cost(5),
+        name="begin",
+    )(half, blocks, vals, rows)
+
+
+def collect_kernel(earlier, started, half_ref, block_ref, vals_hbm, rows_hbm, scale_hbm, *refs):
     count = 2 * earlier
-    rows_hbm, refs = refs[:sources], refs[sources:]
-    before_hbm = refs[:count]
-    high_ref, low_ref, gram_ref, sum_ref, vals_ref, scale_ref = refs[count : count + 6]
-    rows_refs, refs = refs[count + 6 : count + 6 + sources], refs[count + 6 + sources :]
-    before, arrivals = refs[:count], refs[count]
-    slots, width, _ = vals_ref.shape
-    columns = high_ref.shape[1]
-    part = slots // sources
-    half = half_ref[0]
-    starts = [0] if sources == 1 else [half * part, (1 - half) * part]
-    moves = []
-    for i in range(sources):
-        moves.append((vals_hbm.at[pl.ds(starts[i], part)], vals_ref.at[pl.ds(i * part, part)]))
-        moves.append((rows_hbm[i], rows_refs[i]))
-    moves.append((scale_hbm, scale_ref))
+    if started:
+        begun_hbm, refs = refs[0], refs[1:]
+    before_hbm, refs = refs[:count], refs[count:]
+    high_ref, low_ref, gram_ref, sum_ref, whole_ref, vals_ref, rows_ref, scale_ref = refs[:8]
+    before, arrivals = refs[8 : 8 + count], refs[8 + count]
+    begun_ref = refs[9 + count] if started else None
+    part, _, columns = rows_ref.shape
+    first = (1 - half_ref[0]) * part if started else 0
+    moves = [(vals_hbm.at[pl.ds(first, part)], vals_ref), (rows_hbm, rows_ref), (scale_hbm, scale_ref)]
+    if started:
+        moves.append((begun_hbm, begun_ref))
     moves += list(zip(before_hbm, before))
     copies = [pltpu.make_async_copy(src, dst, arrivals.at[i]) for i, (src, dst) in enumerate(moves)]
     for copy in copies:
         copy.start()
     sum_ref[...] = jnp.zeros_like(sum_ref)
-    unroll = 8
-
-    for i in range(sources):
-        copies[2 * i].wait()
-        copies[2 * i + 1].wait()
-
-        def group(g, carry):
-            parts = [
-                jnp.dot(
-                    vals_ref[i * part + g * unroll + u],
-                    rows_refs[i][g * unroll + u],
-                    preferred_element_type=F32,
-                )
-                for u in range(unroll)
-            ]
-            for u in range(unroll):
-                at = pl.multiple_of(block_ref[starts[i] + g * unroll + u] * width, width)
-                sum_ref[pl.ds(at, width), :] += parts[u]
-            return carry
-
-        lax.fori_loop(0, part // unroll, group, 0)
-    for copy in copies[2 * sources :]:
+    for copy in copies[:2]:
         copy.wait()
-    gram_ref[...] = jnp.zeros_like(gram_ref)
+    add_products(sum_ref, vals_ref, rows_ref, block_ref, 0, first, 8)
+    for copy in copies[2:]:
+        copy.wait()
+    whole_ref[...] = jnp.zeros_like(whole_ref)
     step = 512
 
     def tile(t, carry):
         at = pl.ds(pl.multiple_of(t * step, step), step)
         scale = scale_ref[at, :]
-        whole = sum_ref[at, :] * jnp.concatenate([scale] * (columns // LANES), axis=1)
+        whole = sum_ref[at, :]
+        if started:
+            whole = whole + begun_ref[at, :]
+        whole = whole * jnp.concatenate([scale] * (columns // LANES), axis=1)
         high, low = split2(whole)
         high_ref[at, :] = high
         low_ref[at, :] = low
@@ -297,40 +365,52 @@
             else:
                 other_high, other_low = high, low
             wide = other_high.shape[1]
-            gram_ref[:, place : place + wide] += (
+            whole_ref[:, place : place + wide] += (
                 dot(high, other_high, 0, 0) + dot(low, other_high, 0, 0) + dot(high, other_low, 0, 0)
             )
             place += wide
         return carry
 
     lax.fori_loop(0, VOCAB_DEV // step, tile, 0)
-
-
-def collect(half, blocks, vals, scales, rows, before):
-    columns = rows[0].shape[2]
+    known = (whole_ref.shape[1] - columns) // LANES
+    k = 0
+    for r in range(columns // LANES):
+        for c in range(known + r + 1):
+            gram_ref[k] = whole_ref[r * LANES : (r + 1) * LANES, c * LANES : (c + 1) * LANES]
+            k += 1
+
+
+def collect(half, blocks, vals, scales, rows, begun, before):
+    columns = rows.shape[2]
     known = sum(high.shape[1] for high, low in before)
     flat = [piece for pair in before for piece in pair]
-    moved = len(rows) * 2 + 1 + len(flat)
-    return pl.pallas_call(
-        lambda *refs: collect_kernel(len(before), len(rows), *refs),
-        in_specs=[IN_SMEM] * 2 + [IN_HBM] * (2 + len(rows) + len(flat)),
+    extra = [] if begun is None else [begun]
+    rounds = columns // LANES
+    count = sum(known // LANES + r + 1 for r in range(rounds))
+    part = rows.shape[0]
+    return pl.pallas_call(
+        lambda *refs: collect_kernel(len(before), begun is not None, *refs),
+        in_specs=[IN_SMEM] * 2 + [IN_HBM] * (3 + len(extra) + len(flat)),
         out_specs=(FULL_VMEM,) * 3,
         out_shape=(
             jax.ShapeDtypeStruct((VOCAB_DEV, columns), BF16),
             jax.ShapeDtypeStruct((VOCAB_DEV, columns), BF16),
-            jax.ShapeDtypeStruct((columns, known + columns), F32),
+            jax.ShapeDtypeStruct((count, LANES, LANES), F32),
         ),
         scratch_shapes=[
             pltpu.VMEM((VOCAB_DEV, columns), F32),
-            pltpu.VMEM(vals.shape, BF16),
+            pltpu.VMEM((columns, known + columns), F32),
+            pltpu.VMEM((part,) + vals.shape[1:], BF16),
+            pltpu.VMEM(rows.shape, BF16),
             pltpu.VMEM(scales.shape, F32),
         ]
-        + [pltpu.VMEM(piece.shape, BF16) for piece in list(rows) + flat]
-        + [pltpu.SemaphoreType.DMA((moved,))],
+        + [pltpu.VMEM(piece.shape, BF16) for piece in flat]
+        + [pltpu.SemaphoreType.DMA((3 + len(extra) + len(flat),))]
+        + [pltpu.VMEM(piece.shape, F32) for piece in extra],
         compiler_params=params(58),
         cost_estimate=cost(5),
         name="collect",
-    )(half, blocks, vals, scales, *rows, *flat)
+    )(half, blocks, vals, rows, scales, *extra, *flat)
 
 
 def factor_block(rest_ref, unit_ref, upper_ref, inverse_ref):
@@ -341,14 +421,16 @@
     def spread(row):
         return jnp.broadcast_to(row, (8, size))
 
+    def pick(rows, wanted):
+        return spread(jnp.sum(jnp.where(wanted, rows, 0.0), axis=1, keepdims=True))
+
     def panel(p, carry):
+        rows, inverse, left, right = carry[:4]
+        columns = list(carry[4:])
         first = pl.multiple_of(p * 8, 8)
-        rows = rest_ref[pl.ds(first, 8), :]
-        inverse = unit_ref[pl.ds(first, 8), :]
-        columns = [
-            spread(jnp.sum(jnp.where(lane == first + j, rows, 0.0), axis=1, keepdims=True))
-            for j in range(8)
-        ]
+        update = jnp.dot(left, right, preferred_element_type=F32)
+        rest_ref[...] -= update[:, :size]
+        unit_ref[...] -= update[:, size:]
         for j in range(8):
             root = lax.rsqrt(spread(columns[j][j : j + 1, :]))
             lower = columns[j] * root
@@ -362,6 +444,16 @@
         rows = jnp.where(lane >= first + sub, rows, 0.0)
         upper_ref[pl.ds(first, 8), :] = rows
         inverse_ref[pl.ds(first, 8), :] = inverse
+        after = pl.multiple_of(jnp.minimum(first + 8, size - 8), 8)
+        next_rows = rest_ref[pl.ds(after, 8), :]
+        next_inverse = unit_ref[pl.ds(after, 8), :]
+        next_columns = [pick(next_rows, lane == after + j) for j in range(8)]
+        spots = [pick(spread(rows[i : i + 1, :]), lane == after + sub) for i in range(8)]
+        for i in range(8):
+            for j in range(8):
+                next_columns[j] = next_columns[j] - spots[i] * spread(spots[i][j : j + 1, :])
+            next_rows = next_rows - spots[i] * spread(rows[i : i + 1, :])
+            next_inverse = next_inverse - spots[i] * spread(inverse[i : i + 1, :])
         a, b, c = split3(rows)
         x, y, z = split3(inverse)
         left = jnp.concatenate([a, a, b, a, c, b], axis=0).T.astype(BF16)
@@ -369,65 +461,149 @@
             [jnp.concatenate([a, b, a, c, a, b], axis=0), jnp.concatenate([x, y, x, z, x, y], axis=0)],
             axis=1,
         ).astype(BF16)
-        update = jnp.dot(left, right, preferred_element_type=F32)
-        rest_ref[...] -= update[:, :size]
-        unit_ref[...] -= update[:, size:]
-        return carry
-
-    lax.fori_loop(0, size // 8, panel, 0)
-
-
-def cholesky_kernel(row, root, last, count, gram_ref, *refs):
-    refs = list(refs)
-    size = LANES
+        return (next_rows, next_inverse, left, right, *next_columns)
+
+    rows = rest_ref[:8, :]
+    start = (
+        rows,
+        unit_ref[:8, :],
+        jnp.zeros((size, 48), BF16),
+        jnp.zeros((48, 2 * size), BF16),
+        *[pick(rows, lane == j) for j in range(8)],
+    )
+    lax.fori_loop(0, size // 8, panel, start)
+
+
+def gram_block(index, odd_ref, mine_ref, other_ref):
+    half = mine_ref.shape[0]
+    keep = odd_ref[0] == index // half
+    return jnp.where(keep, mine_ref[index % half], other_ref[index % half])
+
+
+def factor_row(first, count, odd_ref, mine_ref, other_ref, known_ref, work):
+    rest_ref, unit_ref, piece_ref, small_ref = work
+    square = (LANES, LANES)
+    corner = gram_block(first + count, odd_ref, mine_ref, other_ref)
+    left = None
     if count:
-        known_ref = refs.pop(0)
-    before = [refs.pop(0) for _ in range(count if last else 0)]
-    inverse_ref, upper_ref, rest_ref, unit_ref, piece_ref, small_ref = refs
-    known = count * size
-    mine = slice(row * size, (row + 1) * size)
-    corner = gram_ref[mine, known : known + size]
-    if count:
-        left = exact(gram_ref[mine, :known], known_ref[...], 1, 1)
+        row = [gram_block(first + k, odd_ref, mine_ref, other_ref) for k in range(count)]
+        left = exact(jnp.concatenate(row, axis=1), known_ref[...], 1, 1)
         corner = corner - exact(left, left, 1, 1)
     rest_ref[...] = corner
-    square = (size, size)
     unit_ref[...] = jnp.where(
         lax.broadcasted_iota(jnp.int32, square, 0) == lax.broadcasted_iota(jnp.int32, square, 1), 1.0, 0.0
     )
     factor_block(rest_ref, unit_ref, piece_ref, small_ref)
     small = small_ref[...]
-    place = known if last else 0
-    if last:
-        upper_ref[...] = jnp.zeros_like(upper_ref)
-        for e in range(count):
-            upper_ref[: (e + 1) * size, e * size : (e + 1) * size] = before[e][...]
+    inverse_row = -exact(small, exact(left, known_ref[...], 1, 0), 1, 0) if count else None
+    return left, small, inverse_row
+
+
+def cholesky_kernel(first, count, root, odd_ref, mine_ref, other_ref, *refs):
+    known_ref = refs[0] if count else None
+    inverse_ref, upper_ref = refs[-6:-4]
+    work = refs[-4:]
+    known = count * LANES
+    left, small, inverse_row = factor_row(first, count, odd_ref, mine_ref, other_ref, known_ref, work)
     if count:
         inverse_ref[:known, :known] = known_ref[...]
-        inverse_ref[:known, known:] = jnp.zeros((known, size), F32)
-        inverse_ref[known:, :known] = -exact(small, exact(left, known_ref[...], 1, 0), 1, 0)
-        upper_ref[:known, place : place + size] = left.T * (1.0 / root)
+        inverse_ref[:known, known:] = jnp.zeros((known, LANES), F32)
+        inverse_ref[known:, :known] = inverse_row
+        upper_ref[:known, :] = left.T * (1.0 / root)
     inverse_ref[known:, known:] = small
-    upper_ref[known:, place : place + size] = piece_ref[...] * (1.0 / root)
-
-
-def cholesky_step(gram, row, inverse, before, root, last):
-    count = len(before)
+    upper_ref[known:, :] = work[2][...] * (1.0 / root)
+
+
+def cholesky_step(odd, halves, first, count, inverse, root):
     total = (count + 1) * LANES
-    inputs = [gram] + ([inverse] if count else []) + (list(before) if last else [])
+    inputs = [odd, *halves] + ([inverse] if count else [])
     square = pltpu.VMEM((LANES, LANES), F32)
     return pl.pallas_call(
-        lambda *refs: cholesky_kernel(row, root, last, count, *refs),
-        in_specs=[FULL_VMEM] * len(inputs),
+        lambda *refs: cholesky_kernel(first, count, root, *refs),
+        in_specs=[IN_SMEM] + [FULL_VMEM] * (len(inputs) - 1),
         out_specs=(FULL_VMEM,) * 2,
         out_shape=(
             jax.ShapeDtypeStruct((total, total), F32),
-            jax.ShapeDtypeStruct((total, total if last else LANES), F32),
+            jax.ShapeDtypeStruct((total, LANES), F32),
         ),
         scratch_shapes=[square] * 4,
         compiler_params=params(16),
         cost_estimate=cost(8),
         name="cholesky_step",
+    )(*inputs)
+
+
+def finish_kernel(first, count, pieces, root, odd_ref, mine_ref, other_ref, known_ref, *refs):
+    before, refs = refs[:count], refs[count:]
+    pieces_hbm, refs = refs[: 2 * pieces], refs[2 * pieces + 1 :]
+    basis_hbm, upper_ref = refs[:2]
+    work = refs[2:6]
+    stage_ref, arrivals, departures = refs[6:9]
+    held = refs[9:]
+    known = count * LANES
+    copies = [
+        pltpu.make_async_copy(src, dst, arrivals.at[i]) for i, (src, dst) in enumerate(zip(pieces_hbm, held))
+    ]
+    for copy in copies:
+        copy.start()
+    left, small, inverse_row = factor_row(first, count, odd_ref, mine_ref, other_ref, known_ref, work)
+    row_high, row_low = split2(jnp.concatenate([inverse_row, small], axis=1))
+    for copy in copies:
+        copy.wait()
+    steps, step = stage_ref.shape[:2]
+    sent = []
+    for t in range(steps):
+        at = slice(t * step, (t + 1) * step)
+        total = None
+        place = 0
+        for e in range(pieces):
+            high, low = held[2 * e][at, :], held[2 * e + 1][at, :]
+            wide = high.shape[1]
+            high_part, low_part = row_high[:, place : place + wide], row_low[:, place : place + wide]
+            term = dot(high, high_part, 1, 1) + dot(low, high_part, 1, 1) + dot(high, low_part, 1, 1)
+            total = term if total is None else total + term
+            place += wide
+        stage_ref[t] = total * root
+        copy = pltpu.make_async_copy(
+            stage_ref.at[t], basis_hbm.at[pl.ds(t * step, step), pl.ds(known, LANES)], departures.at[t]
+        )
+        copy.start()
+        sent.append(copy)
+    upper_ref[...] = jnp.zeros_like(upper_ref)
+    for e in range(count):
+        upper_ref[: (e + 1) * LANES, e * LANES : (e + 1) * LANES] = before[e][...]
+    upper_ref[:known, known:] = left.T * (1.0 / root)
+    upper_ref[known:, known:] = work[2][...] * (1.0 / root)
+    for copy in sent:
+        copy.wait()
+
+
+def finish(odd, halves, first, inverse, before, pieces, basis, root):
+    count = len(before)
+    total = (count + 1) * LANES
+    flat = [piece for pair in pieces for piece in pair]
+    inputs = [odd, *halves, inverse, *before, *flat, basis]
+    steps = 4
+    square = pltpu.VMEM((LANES, LANES), F32)
+    return pl.pallas_call(
+        lambda *refs: finish_kernel(first, count, len(pieces), root, *refs),
+        in_specs=[IN_SMEM] + [FULL_VMEM] * (3 + count) + [IN_HBM] * (len(flat) + 1),
+        out_specs=(IN_HBM, FULL_VMEM),
+        out_shape=(
+            jax.ShapeDtypeStruct(basis.shape, F32),
+            jax.ShapeDtypeStruct((total, total), F32),
+        ),
+        scratch_shapes=[square] * 4
+        + [
+            pltpu.VMEM((steps, VOCAB_DEV // steps, LANES), F32),
+            pltpu.SemaphoreType.DMA((len(flat),)),
+            pltpu.SemaphoreType.DMA((steps,)),
+        ]
+        + [pltpu.VMEM(piece.shape, BF16) for piece in flat],
+        input_output_aliases={len(inputs) - 1: 0},
+        compiler_params=params(58),
+        cost_estimate=cost(12),
+        name="finish",
     )(*inputs)
 
 
@@ -483,8 +659,8 @@
 
 
 def sum_all(x):
-    for axis in ("docs", "rest", "half"):
-        for bit in bits(axis):
+    for axis in ("half", "rest", "docs"):
+        for bit in reversed(bits(axis)):
             x = x + swap(x, axis, bit)
     return x
 
@@ -500,9 +676,7 @@
             if axis != "docs" or bit > 1:
                 mine = mine + swap(mine, axis, bit)
     other = swap(mine, "docs", 1)
-    return jnp.concatenate(
-        [jnp.where(odd == 0, mine, other), jnp.where(odd == 0, other, mine)], axis=0
-    )
+    return mine, other
 
 
 def body(images, sketch, tile_vals, tile_rows, tile_count, tile_block):
@@ -528,9 +702,8 @@
     root = math.sqrt(VOCAB_DEV * senders)
     scale, turned = row_scales(blocks, vals)
     where = half.reshape(1).astype(jnp.int32)
-    table, last_table = project(power, images, sketch, doc_rows * senders, cut)
+    table, last_table, near = project(power, near_index, images, sketch, doc_rows * senders, cut)
     far_table = swap(table, "half", 1)
-    near = gather_rows(near_index, table)
     near = lax.all_to_all(near, SIDE, 0, 0, tiled=True)
     far = gather_rows(far_index, far_table)
     far = lax.all_to_all(far, SIDE, 0, 0, tiled=True)
@@ -540,18 +713,23 @@
     def by_slot(rows):
         return rows.reshape(-1, tile_height, rows.shape[2])
 
+    odd = (lax.axis_index("docs") % 2).reshape(1).astype(jnp.int32)
+    begun = begin(where, blocks, turned, by_slot(near))
     pieces, uppers = [], []
     inverse = basis = None
-    for rows in [[by_slot(near), by_slot(far)], [by_slot(final)]]:
-        high, low, gram = collect(where, blocks, turned, scale, rows, pieces)
+    for c, rows in enumerate([by_slot(far), by_slot(final)]):
+        high, low, gram = collect(where, blocks, turned, scale, rows, begun if c == 0 else None, pieces)
         pieces.append((high, low))
-        gram = sum_halves(gram)
-        for row in range(gram.shape[0] // LANES):
-            last = (len(uppers) + 1) * LANES == columns
-            inverse, upper = cholesky_step(gram, row, inverse, uppers, root, last)
+        grams = sum_halves(gram)
+        first = 0
+        for _ in range(high.shape[1] // LANES):
+            count = len(uppers)
+            if (count + 1) * LANES == columns:
+                return finish(odd, grams, first, inverse, uppers, pieces, basis, root)
+            inverse, upper = cholesky_step(odd, grams, first, count, inverse, root)
             uppers.append(upper)
+            first += count + 1
         basis = basis_block(inverse, pieces, basis, root, columns)
-    return (basis, uppers[-1])
 
 
 def solution(mesh):

time: 258 us -> 253 us (0.981)
  Pallas kernels: 99 us -> 91.1 us
  waiting for transfers between devices: 102 us -> 109 us
  starting transfers between devices: 43.2 us -> 40 us
    ppermute x19, waiting for transfers between devices: 83.8 us -> 93.3 us  [swap(): return lax.ppermute(x, axis, [(i, i ^ bit) for i in range(size)])]
    pallas_call x2 -> x1, Pallas kernels: 12.1 us -> 6.36 us  [basis_block(): pl.pallas_call(lambda *refs: basis_kernel(len(pieces), known, root, *refs...]
    pallas_call x3 -> x2, Pallas kernels: 16.4 us -> 11.4 us  [gather_rows(): pl.pallas_call(gather_kernel, grid=(senders // group,), in_specs=[pl.Bloc...]
    ppermute x19, starting transfers between devices: 23.3 us -> 20.1 us  [swap(): return lax.ppermute(x, axis, [(i, i ^ bit) for i in range(size)])]
    pallas_call x7 -> x8, Pallas kernels: 57.2 us -> 60 us  [the longest x3 16.4 us: cholesky_step(): pl.pallas_call(lambda *refs: cholesky_kernel(first, count, root, *refs),...]
    all_to_all x1, waiting for transfers between devices: 2.64 us -> 0.01 us  [body(): final = lax.all_to_all(final, BOTH, 0, 0, tiled=True)]
  transfers between devices with their start and end apart: 23 -> 23, of which waited for: 16 -> 14; matrix products, arithmetic and copies ran while one was open for 3% -> 3% of each run, Pallas kernels for 20% -> 29%
where the time goes in v2:
time: 253 us; the launch traced here: 252 us
  waiting for transfers between devices  109 us (43%)
  Pallas kernels  91.1 us (36%)
  starting transfers between devices  40 us (16%)
  local copies, waits for them, and re-layouts  8.65 us (3%)
  other arithmetic  2.71 us (1%)
    ppermute x19, waiting for transfers between devices, swap(): return lax.ppermute(x, axis, [(i, i ^ bit) for i in range(size)])  93.3 us
    ppermute x19, starting transfers between devices, swap(): return lax.ppermute(x, axis, [(i, i ^ bit) for i in range(size)])  20.1 us
    pallas_call x3, Pallas kernels, cholesky_step(): pl.pallas_call(lambda *refs: cholesky_kernel(first, count, root, *refs),...  16.4 us
    pallas_call x2, Pallas kernels, collect(): pl.pallas_call(lambda *refs: collect_kernel(len(before), begun is not Non...  15.6 us
    all_to_all x1, waiting for transfers between devices, body(): far = lax.all_to_all(far, SIDE, 0, 0, tiled=True)  15.4 us
    pallas_call x1, Pallas kernels, finish(): pl.pallas_call(lambda *refs: finish_kernel(first, count, len(pieces), roo...  11.6 us
    pallas_call x2, Pallas kernels, gather_rows(): pl.pallas_call(gather_kernel, grid=(senders // group,), in_specs=[pl.Bloc...  11.4 us
    pallas_call x1, Pallas kernels, project(): pl.pallas_call(lambda *refs: project_kernel(documents, steps, group, *ref...  11.1 us
  transfers between devices with their start and end apart: 23, of which 14 were waited for; matrix products, arithmetic and copies ran while one was open for 3% of the time, Pallas kernels for 29%

profile of v2, /device:TPU:0, one launch (start us, length us, event | category | flops | bytes accessed | tf_op | source)
XLA Modules:
  0.0 252.3 jit_solution(3921566144223525517)
XLA Ops:
  0.6 5.8 %prepare.1 = (bf16[32,2,64,128]{3,2,1,0:T(8,128)(2,1)}, f32[1,4096]{1,0:T(1,128)}) custom-call(s32[1,32]{1,0:T(1,128)} %refs_0_.1, bf16[1024,4096]{1,0:T(8,128)(2,1)} %refs_2_.3, bf16[1,32,2,64,128]{4,3,2,1,0:T(8,128)(2,1)} %refs_2_.2), custom_call_target="tpu_custom_call" | custom-call | flops 4000000000 | tf_op jit(solution)/shard_map/prepare/pallas_call | solution.py:92
  6.4 7.3 %all-to-all-start = ((bf16[32,128,128]{2,1,0:T(8,128)(2,1)}), bf16[32,128,128]{2,1,0:T(8,128)(2,1)S(1)}, u32[]{:S(2)}, u32[]{:S(2)}) async-start(bf16[32,128,128]{2,1,0:T(8,128)(2,1)} %bitcast.15), calls=%async_computation | async-start | bytes 2097152 | tf_op jit(solution)/shard_map/all_to_all | solution.py:692
  16.5 24.2 %collective-permute-done = f32[1,4096]{1,0:T(1,128)S(1)} collective-permute-done((f32[1,4096]{1,0:T(1,128)S(1)}, f32[1,4096]{1,0:T(1,128)S(1)}, u32[]{:S(2)}, u32[]{:S(2)}) %collective-permute-start) | collective-permute-done | bytes 16416 | tf_op jit(solution)/shard_map/ppermute | solution.py:653
  54.1 11.1 %project.1 = (bf16[1024,384]{1,0:T(8,128)(2,1)}, bf16[1024,128]{1,0:T(8,128)(2,1)}, bf16[16,128,384]{2,1,0:T(8,128)(2,1)}) custom-call(f32[1,4096]{1,0:T(1,128)} %add.76.refs_0_, s32[16,1,128]{2,1,0:T(1,128)} %bitcast.16, bf16[1024,4096]{1,0:T(8,128)(2,1)} %refs_2_.3, bf16[4096,512]{1,0:T(8,128)(2,1)} %refs_3_.1), custom_call_target="tpu_custom_call" | custom-call | flops 8999999488 | tf_op jit(solution)/shard_map/project/pallas_call | solution.py:193
  65.2 3.8 %all-to-all-start.3 = ((bf16[16,128,384]{2,1,0:T(8,128)(2,1)}), bf16[16,128,384]{2,1,0:T(8,128)(2,1)S(1)}, u32[]{:S(2)}, u32[]{:S(2)}) async-start(bf16[16,128,384]{2,1,0:T(8,128)(2,1)} %get-tuple-element.27), calls=%async_computation.3 | async-start | bytes 3145728 | tf_op jit(solution)/shard_map/all_to_all | solution.py:707
  72.0 35.2 %collective-permute-done.5 = s32[16,128]{1,0:T(8,128)S(1)} collective-permute-done((s32[16,128]{1,0:T(8,128)S(1)}, s32[16,128]{1,0:T(8,128)S(1)}, u32[]{:S(2)}, u32[]{:S(2)}) %collective-permute-start.5) | collective-permute-done | bytes 8224 | tf_op jit(solution)/shard_map/ppermute | solution.py:653
  108.1 5.0 %gather_rows.3 = bf16[16,128,384]{2,1,0:T(8,128)(2,1)} custom-call(s32[16,1,128]{2,1,0:T(1,128)} %bitcast.17, bf16[1024,384]{1,0:T(8,128)(2,1)} %copy-done.12), custom_call_target="tpu_custom_call" | custom-call | flops 3000000000 | tf_op jit(solution)/shard_map/gather_rows/pallas_call | solution.py:237
  113.1 4.1 %all-to-all-start.2 = ((bf16[16,128,384]{2,1,0:T(8,128)(2,1)}), bf16[16,128,384]{2,1,0:T(8,128)(2,1)S(1)}, u32[]{:S(2)}, u32[]{:S(2)}) async-start(bf16[16,128,384]{2,1,0:T(8,128)(2,1)} %gather_rows.3), calls=%async_computation.2 | async-start | bytes 3145728 | tf_op jit(solution)/shard_map/all_to_all | solution.py:709
  118.0 6.4 %gather_rows.2 = bf16[32,128,128]{2,1,0:T(8,128)(2,1)} custom-call(s32[32,1,128]{2,1,0:T(1,128)} %reshape_reshape_squeeze.6.index_ref, bf16[1024,128]{1,0:T(8,128)(2,1)} %get-tuple-element.24.table_ref), custom_call_target="tpu_custom_call" | custom-call | flops 3000000000 | tf_op jit(solution)/shard_map/gather_rows/pallas_call | solution.py:237
  124.4 15.4 %all-to-all-done.2 = bf16[16,128,384]{2,1,0:T(8,128)(2,1)S(1)} async-done(((bf16[16,128,384]{2,1,0:T(8,128)(2,1)}), bf16[16,128,384]{2,1,0:T(8,128)(2,1)S(1)}, u32[]{:S(2)}, u32[]{:S(2)}) %all-to-all-start.2) | async-done | bytes 1572896 | tf_op jit(solution)/shard_map/all_to_all | solution.py:709
  139.8 4.7 %all-to-all-start.1 = ((bf16[32,128,128]{2,1,0:T(8,128)(2,1)}), bf16[32,128,128]{2,1,0:T(8,128)(2,1)S(1)}, u32[]{:S(2)}, u32[]{:S(2)}) async-start(bf16[32,128,128]{2,1,0:T(8,128)(2,1)} %gather_rows.2), calls=%async_computation.1 | async-start | bytes 2097152 | tf_op jit(solution)/shard_map/all_to_all | solution.py:711
  145.2 7.5 %row_scales.1 = (f32[2048,128]{1,0:T(8,128)}, bf16[64,128,64]{2,1,0:T(8,128)(2,1)}) custom-call(s32[64]{0:T(128)} %reshape_squeeze.3.block_ref.refs_1_, bf16[64,64,128]{2,1,0:T(8,128)(2,1)} %bitcast.13), custom_call_target="tpu_custom_call" | custom-call | flops 3000000000 | tf_op jit(solution)/shard_map/row_scales/pallas_call | solution.py:272
  152.6 5.3 %begin.1.refs_5_ = f32[2048,384]{1,0:T(8,128)} custom-call(s32[1]{0:T(128)} %bitcast.1.half_ref.refs_0_, s32[64]{0:T(128)} %reshape_squeeze.3.block_ref.refs_1_, bf16[64,128,64]{2,1,0:T(8,128)(2,1)} %get-tuple-element.22.vals_ref.refs_2_, bf16[32,64,384]{2,1,0:T(8,128)(2,1)} %bitcast.11), custom_call_target="tpu_custom_call" | custom-call | flops 5000000000 | tf_op jit(solution)/shard_map/begin/pallas_call | solution.py:314
  157.9 8.5 %collect.2 = (bf16[2048,384]{1,0:T(8,128)(2,1)}, bf16[2048,384]{1,0:T(8,128)(2,1)}, f32[6,128,128]{2,1,0:T(8,128)}) custom-call(s32[1]{0:T(128)} %bitcast.1.half_ref.refs_0_, s32[64]{0:T(128)} %reshape_squeeze.3.block_ref.refs_1_, bf16[64,128,64]{2,1,0:T(8,128)(2,1)} %get-tuple-element.22.vals_ref.refs_2_, bf16[32,64,384]{2,1,0:T(8,128)(2,1)} %bitcast.12, ...), custom_call_target="tpu_custom_call" | custom-call | flops 5000000000 | tf_op jit(solution)/shard_map/collect/pallas_call | solution.py:391
  172.5 7.2 %collect.3 = (bf16[2048,128]{1,0:T(8,128)(2,1)}, bf16[2048,128]{1,0:T(8,128)(2,1)}, f32[4,128,128]{2,1,0:T(8,128)}) custom-call(s32[1]{0:T(128)} %bitcast.1.half_ref.refs_0_, s32[64]{0:T(128)} %reshape_squeeze.3.block_ref.refs_1_, bf16[64,128,64]{2,1,0:T(8,128)(2,1)} %get-tuple-element.22.vals_ref.refs_2_, bf16[64,64,128]{2,1,0:T(8,128)(2,1)} %bitcast.14, ...), custom_call_target="tpu_custom_call" | custom-call | flops 5000000000 | tf_op jit(solution)/shard_map/collect/pallas_call | solution.py:391
  182.2 4.2 %collective-permute-done.15 = f32[3,128,128]{2,1,0:T(8,128)S(1)} collective-permute-done((f32[3,128,128]{2,1,0:T(8,128)S(1)}, f32[3,128,128]{2,1,0:T(8,128)S(1)}, u32[]{:S(2)}, u32[]{:S(2)}) %collective-permute-start.15) | collective-permute-done | bytes 196640 | tf_op jit(solution)/shard_map/ppermute | solution.py:653
  189.5 4.4 %collective-permute-done.8 = f32[2,128,128]{2,1,0:T(8,128)S(1)} collective-permute-done((f32[2,128,128]{2,1,0:T(8,128)S(1)}, f32[2,128,128]{2,1,0:T(8,128)S(1)}, u32[]{:S(2)}, u32[]{:S(2)}) %collective-permute-start.8) | collective-permute-done | bytes 131104 | tf_op jit(solution)/shard_map/ppermute | solution.py:653
  199.6 5.6 %collective-permute-done.17 = f32[3,128,128]{2,1,0:T(8,128)S(1)} collective-permute-done((f32[3,128,128]{2,1,0:T(8,128)S(1)}, f32[3,128,128]{2,1,0:T(8,128)S(1)}, u32[]{:S(2)}, u32[]{:S(2)}) %collective-permute-start.17) | collective-permute-done | bytes 196640 | tf_op jit(solution)/shard_map/ppermute | solution.py:653
  206.5 8.2 %collective-permute-done.11 = f32[2,128,128]{2,1,0:T(8,128)S(1)} collective-permute-done((f32[2,128,128]{2,1,0:T(8,128)S(1)}, f32[2,128,128]{2,1,0:T(8,128)S(1)}, u32[]{:S(2)}, u32[]{:S(2)}) %collective-permute-start.11) | collective-permute-done | bytes 131104 | tf_op jit(solution)/shard_map/ppermute | solution.py:653
  214.9 4.6 %cholesky_step.3 = (f32[128,128]{1,0:T(8,128)S(1)}, f32[128,128]{1,0:T(8,128)S(1)}) custom-call(s32[1]{0:T(128)} %bitcast.refs_0_, f32[3,128,128]{2,1,0:T(8,128)S(1)} %add.92.refs_1_, f32[3,128,128]{2,1,0:T(8,128)S(1)} %collective-permute-done.18.refs_2_), custom_call_target="tpu_custom_call" | custom-call | flops 8000000000 | tf_op jit(solution)/shard_map/cholesky_step/pallas_call | solution.py:521
  220.1 5.7 %cholesky_step.4 = (f32[256,256]{1,0:T(8,128)S(1)}, f32[256,128]{1,0:T(8,128)S(1)}) custom-call(s32[1]{0:T(128)} %bitcast.refs_0_, f32[3,128,128]{2,1,0:T(8,128)S(1)} %add.92.refs_1_, f32[3,128,128]{2,1,0:T(8,128)S(1)} %collective-permute-done.18.refs_2_, f32[128,128]{1,0:T(8,128)S(1)} %get-tuple-element.32.refs_3_), custom_call_target="tpu_custom_call" | custom-call | flops 8000000000 | tf_op jit(solution)/shard_map/cholesky_step/pallas_call | solution.py:521
  225.9 6.1 %cholesky_step.5 = (f32[384,384]{1,0:T(8,128)S(1)}, f32[384,128]{1,0:T(8,128)S(1)}) custom-call(s32[1]{0:T(128)} %bitcast.refs_0_, f32[3,128,128]{2,1,0:T(8,128)S(1)} %add.92.refs_1_, f32[3,128,128]{2,1,0:T(8,128)S(1)} %collective-permute-done.18.refs_2_, f32[256,256]{1,0:T(8,128)S(1)} %get-tuple-element.33.refs_3_), custom_call_target="tpu_custom_call" | custom-call | flops 8000000000 | tf_op jit(solution)/shard_map/cholesky_step/pallas_call | solution.py:521
  233.4 6.4 %basis_block.1.refs_11_ = f32[2048,512]{1,0:T(8,128)} custom-call(f32[384,384]{1,0:T(8,128)} %copy-done, bf16[2048,384]{1,0:T(8,128)(2,1)} %get-tuple-element.28.refs_5_.refs_1_.refs_7_, bf16[2048,384]{1,0:T(8,128)(2,1)} %get-tuple-element.29.refs_6_.refs_2_.refs_8_), custom_call_target="tpu_custom_call" | custom-call | flops 3000000000 | tf_op jit(solution)/shard_map/basis_block/pallas_call | solution.py:638
  240.5 11.6 %finish.1 = (f32[2048,512]{1,0:T(8,128)}, f32[512,512]{1,0:T(8,128)}) custom-call(s32[1]{0:T(128)} %bitcast.refs_0_, f32[2,128,128]{2,1,0:T(8,128)} %copy-done.8, f32[2,128,128]{2,1,0:T(8,128)} %copy-done.13, f32[384,384]{1,0:T(8,128)} %copy-done, f32[128,128]{1,0:T(8,128)} %copy-done.3, f32[256,128]{1,0:T(8,128)} %copy-done.2, ...), custom_call_target="tpu_custom_call", output_to_operand_aliasing={{0}: (11, {})} | custom-call | flops 12000000000 | tf_op jit(solution)/shard_map/finish/pallas_call | solution.py:588
  (87 shorter events, 43.0 us)
Async XLA Ops:
  6.4 58.7 %all-to-all-start = ((bf16[32,128,128]{2,1,0:T(8,128)(2,1)}), bf16[32,128,128]{2,1,0:T(8,128)(2,1)S(1)}, u32[]{:S(2)}, u32[]{:S(2)}) async-start(bf16[32,128,128]{2,1,0:T(8,128)(2,1)} %bitcast.15), calls=%async_computation | async-start | bytes 2097152 | tf_op jit(solution)/shard_map/all_to_all | solution.py:692
  13.8 26.9 %collective-permute-start = (f32[1,4096]{1,0:T(1,128)S(1)}, f32[1,4096]{1,0:T(1,128)S(1)}, u32[]{:S(2)}, u32[]{:S(2)}) collective-permute-start(f32[1,4096]{1,0:T(1,128)S(1)} %copy-done.10), channel_id=1, source_target_pairs={{0,16},{16,0},{1,17},{17,1},{2,18},{18,2},{3,19},{19,3},{4,20},{20... | collective-permute-start | bytes 49160 | tf_op jit(solution)/shard_map/ppermute | solution.py:653
  40.7 3.8 %collective-permute-start.1 = (f32[1,4096]{1,0:T(1,128)S(1)}, f32[1,4096]{1,0:T(1,128)S(1)}, u32[]{:S(2)}, u32[]{:S(2)}) collective-permute-start(f32[1,4096]{1,0:T(1,128)S(1)} %add.72), channel_id=1, source_target_pairs={{0,8},{4,12},{8,0},{12,4},{1,9},{5,13},{9,1},{13,5},{2,10},{6,14},... | collective-permute-start | bytes 49160 | tf_op jit(solution)/shard_map/ppermute | solution.py:653
  44.5 3.8 %collective-permute-start.2 = (f32[1,4096]{1,0:T(1,128)S(1)}, f32[1,4096]{1,0:T(1,128)S(1)}, u32[]{:S(2)}, u32[]{:S(2)}) collective-permute-start(f32[1,4096]{1,0:T(1,128)S(1)} %add.73), channel_id=1, source_target_pairs={{0,4},{4,0},{8,12},{12,8},{1,5},{5,1},{9,13},{13,9},{2,6},{6,2},{1... | collective-permute-start | bytes 49160 | tf_op jit(solution)/shard_map/ppermute | solution.py:653
  48.4 3.8 %collective-permute-start.3 = (f32[1,4096]{1,0:T(1,128)S(1)}, f32[1,4096]{1,0:T(1,128)S(1)}, u32[]{:S(2)}, u32[]{:S(2)}) collective-permute-start(f32[1,4096]{1,0:T(1,128)S(1)} %add.74), channel_id=1, source_target_pairs={{0,2},{1,3},{2,0},{3,1},{4,6},{5,7},{6,4},{7,5},{8,10},{9,11},{10,... | collective-permute-start | bytes 49160 | tf_op jit(solution)/shard_map/ppermute | solution.py:653
  52.2 1.2 collective-permute-start.4
  65.2 47.9 %copy-start.6 = (bf16[32,128,128]{2,1,0:T(8,128)(2,1)}, bf16[32,128,128]{2,1,0:T(8,128)(2,1)S(1)}, u32[]{:S(2)}) copy-start(bf16[32,128,128]{2,1,0:T(8,128)(2,1)S(1)} %all-to-all-done) | copy-start | bytes 3145732
  65.2 47.9 %all-to-all-start.3 = ((bf16[16,128,384]{2,1,0:T(8,128)(2,1)}), bf16[16,128,384]{2,1,0:T(8,128)(2,1)S(1)}, u32[]{:S(2)}, u32[]{:S(2)}) async-start(bf16[16,128,384]{2,1,0:T(8,128)(2,1)} %get-tuple-element.27), calls=%async_computation.3 | async-start | bytes 3145728 | tf_op jit(solution)/shard_map/all_to_all | solution.py:707
  69.0 38.2 %collective-permute-start.6 = (bf16[1024,384]{1,0:T(8,128)(2,1)}, bf16[1024,384]{1,0:T(8,128)(2,1)S(1)}, u32[]{:S(2)}, u32[]{:S(2)}) collective-permute-start(bf16[1024,384]{1,0:T(8,128)(2,1)} %get-tuple-element.26), channel_id=1, source_target_pairs={{0,16},{16,0},{1,17},{17,1},{2,18},{18,2},{3,19},{19,3},{4,20},{20... | collective-permute-start | bytes 2359304 | tf_op jit(solution)/shard_map/ppermute | solution.py:653
  70.5 36.7 %collective-permute-start.5 = (s32[16,128]{1,0:T(8,128)S(1)}, s32[16,128]{1,0:T(8,128)S(1)}, u32[]{:S(2)}, u32[]{:S(2)}) collective-permute-start(s32[16,128]{1,0:T(8,128)S(1)} %get-tuple-element.40), channel_id=1, source_target_pairs={{0,16},{16,0},{1,17},{17,1},{2,18},{18,2},{3,19},{19,3},{4,20},{20... | collective-permute-start | bytes 24584 | tf_op jit(solution)/shard_map/ppermute | solution.py:653
  113.1 26.6 %all-to-all-start.2 = ((bf16[16,128,384]{2,1,0:T(8,128)(2,1)}), bf16[16,128,384]{2,1,0:T(8,128)(2,1)S(1)}, u32[]{:S(2)}, u32[]{:S(2)}) async-start(bf16[16,128,384]{2,1,0:T(8,128)(2,1)} %gather_rows.3), calls=%async_computation.2 | async-start | bytes 3145728 | tf_op jit(solution)/shard_map/all_to_all | solution.py:709
  139.8 31.7 %all-to-all-start.1 = ((bf16[32,128,128]{2,1,0:T(8,128)(2,1)}), bf16[32,128,128]{2,1,0:T(8,128)(2,1)S(1)}, u32[]{:S(2)}, u32[]{:S(2)}) async-start(bf16[32,128,128]{2,1,0:T(8,128)(2,1)} %gather_rows.2), calls=%async_computation.1 | async-start | bytes 2097152 | tf_op jit(solution)/shard_map/all_to_all | solution.py:711
  167.4 1.5 collective-permute-start.13
  169.8 9.8 %collective-permute-start.14 = (f32[3,128,128]{2,1,0:T(8,128)S(1)}, f32[3,128,128]{2,1,0:T(8,128)S(1)}, u32[]{:S(2)}, u32[]{:S(2)}) collective-permute-start(f32[3,128,128]{2,1,0:T(8,128)S(1)} %dynamic-slice_add_fusion), channel_id=1, source_target_pairs={{0,2},{1,3},{2,0},{3,1},{4,6},{5,7},{6,4},{7,5},{8,10},{9,11},{10,... | collective-permute-start | bytes 589832 | tf_op jit(solution)/shard_map/ppermute | solution.py:653
  179.7 6.7 %collective-permute-start.15 = (f32[3,128,128]{2,1,0:T(8,128)S(1)}, f32[3,128,128]{2,1,0:T(8,128)S(1)}, u32[]{:S(2)}, u32[]{:S(2)}) collective-permute-start(f32[3,128,128]{2,1,0:T(8,128)S(1)} %add.89), channel_id=1, source_target_pairs={{0,4},{4,0},{8,12},{12,8},{1,5},{5,1},{9,13},{13,9},{2,6},{6,2},{1... | collective-permute-start | bytes 589832 | tf_op jit(solution)/shard_map/ppermute | solution.py:653
  182.1 5.8 %collective-permute-start.7 = (f32[2,128,128]{2,1,0:T(8,128)S(1)}, f32[2,128,128]{2,1,0:T(8,128)S(1)}, u32[]{:S(2)}, u32[]{:S(2)}) collective-permute-start(f32[2,128,128]{2,1,0:T(8,128)S(1)} %constant_dynamic-slice_fusion.1), channel_id=1, source_target_pairs={{0,1},{1,0},{2,3},{3,2},{4,5},{5,4},{6,7},{7,6},{8,9},{9,8},{10,11... | collective-permute-start | bytes 393224 | tf_op jit(solution)/shard_map/ppermute | solution.py:653
  186.4 9.1 %collective-permute-start.16 = (f32[3,128,128]{2,1,0:T(8,128)S(1)}, f32[3,128,128]{2,1,0:T(8,128)S(1)}, u32[]{:S(2)}, u32[]{:S(2)}) collective-permute-start(f32[3,128,128]{2,1,0:T(8,128)S(1)} %add.90), channel_id=1, source_target_pairs={{0,8},{4,12},{8,0},{12,4},{1,9},{5,13},{9,1},{13,5},{2,10},{6,14},... | collective-permute-start | bytes 589832 | tf_op jit(solution)/shard_map/ppermute | solution.py:653
  188.9 5.0 %collective-permute-start.8 = (f32[2,128,128]{2,1,0:T(8,128)S(1)}, f32[2,128,128]{2,1,0:T(8,128)S(1)}, u32[]{:S(2)}, u32[]{:S(2)}) collective-permute-start(f32[2,128,128]{2,1,0:T(8,128)S(1)} %dynamic-slice_add_fusion.1), channel_id=1, source_target_pairs={{0,2},{1,3},{2,0},{3,1},{4,6},{5,7},{6,4},{7,5},{8,10},{9,11},{10,... | collective-permute-start | bytes 393224 | tf_op jit(solution)/shard_map/ppermute | solution.py:653
  193.9 5.0 %collective-permute-start.9 = (f32[2,128,128]{2,1,0:T(8,128)S(1)}, f32[2,128,128]{2,1,0:T(8,128)S(1)}, u32[]{:S(2)}, u32[]{:S(2)}) collective-permute-start(f32[2,128,128]{2,1,0:T(8,128)S(1)} %add.82), channel_id=1, source_target_pairs={{0,4},{4,0},{8,12},{12,8},{1,5},{5,1},{9,13},{13,9},{2,6},{6,2},{1... | collective-permute-start | bytes 393224 | tf_op jit(solution)/shard_map/ppermute | solution.py:653
  195.5 9.7 %collective-permute-start.17 = (f32[3,128,128]{2,1,0:T(8,128)S(1)}, f32[3,128,128]{2,1,0:T(8,128)S(1)}, u32[]{:S(2)}, u32[]{:S(2)}) collective-permute-start(f32[3,128,128]{2,1,0:T(8,128)S(1)} %add.91), channel_id=1, source_target_pairs={{0,16},{16,0},{1,17},{17,1},{2,18},{18,2},{3,19},{19,3},{4,20},{20... | collective-permute-start | bytes 589832 | tf_op jit(solution)/shard_map/ppermute | solution.py:653
  199.0 6.8 %collective-permute-start.10 = (f32[2,128,128]{2,1,0:T(8,128)S(1)}, f32[2,128,128]{2,1,0:T(8,128)S(1)}, u32[]{:S(2)}, u32[]{:S(2)}) collective-permute-start(f32[2,128,128]{2,1,0:T(8,128)S(1)} %add.83), channel_id=1, source_target_pairs={{0,8},{4,12},{8,0},{12,4},{1,9},{5,13},{9,1},{13,5},{2,10},{6,14},... | collective-permute-start | bytes 393224 | tf_op jit(solution)/shard_map/ppermute | solution.py:653
  205.2 9.7 %collective-permute-start.18 = (f32[3,128,128]{2,1,0:T(8,128)S(1)}, f32[3,128,128]{2,1,0:T(8,128)S(1)}, u32[]{:S(2)}, u32[]{:S(2)}) collective-permute-start(f32[3,128,128]{2,1,0:T(8,128)S(1)} %add.92.refs_1_), channel_id=1, source_target_pairs={{0,1},{1,0},{2,3},{3,2},{4,5},{5,4},{6,7},{7,6},{8,9},{9,8},{10,11... | collective-permute-start | bytes 589832 | tf_op jit(solution)/shard_map/ppermute | solution.py:653
  205.8 9.0 %collective-permute-start.11 = (f32[2,128,128]{2,1,0:T(8,128)S(1)}, f32[2,128,128]{2,1,0:T(8,128)S(1)}, u32[]{:S(2)}, u32[]{:S(2)}) collective-permute-start(f32[2,128,128]{2,1,0:T(8,128)S(1)} %add.84), channel_id=1, source_target_pairs={{0,16},{16,0},{1,17},{17,1},{2,18},{18,2},{3,19},{19,3},{4,20},{20... | collective-permute-start | bytes 393224 | tf_op jit(solution)/shard_map/ppermute | solution.py:653
  214.8 25.0 %collective-permute-start.12 = (f32[2,128,128]{2,1,0:T(8,128)S(1)}, f32[2,128,128]{2,1,0:T(8,128)S(1)}, u32[]{:S(2)}, u32[]{:S(2)}) collective-permute-start(f32[2,128,128]{2,1,0:T(8,128)S(1)} %add.85.refs_1_), channel_id=1, source_target_pairs={{0,1},{1,0},{2,3},{3,2},{4,5},{5,4},{6,7},{7,6},{8,9},{9,8},{10,11... | collective-permute-start | bytes 393224 | tf_op jit(solution)/shard_map/ppermute | solution.py:653
  (14 other events, 111.1 us)
